TPU v7x, 256 devices: a whole 4x4x8 slice. The times are simulated.
256 devices in a mesh: replica: 16 (over z, core), model: 4 (over x), shift: 4 (over y).
Axes of the slice: x: 4, y: 4, z: 8, core: 2. Of those that a mesh axis runs over, the one named last changes fastest.
Arguments:
- partial_gate: float32 [64, 1024, 3072], P(('shift', 'replica'), None, 'model'), parts along dimension 0, may hold values from -0.875 to 0.875
- partial_up: float32 [64, 1024, 3072], P(('shift', 'replica'), None, 'model'), parts along dimension 0, may hold values from -0.875 to 0.875
- partial_down: float32 [64, 3072, 1024], P(('shift', 'replica'), 'model'), parts along dimension 0, may hold values from -0.875 to 0.875
- partial_norm: float32 [64, 1024], P(('shift', 'replica')), parts along dimension 0, may hold values from -8 to 8
- master_gate: float32 [4096, 3072], P(('shift', 'replica'), 'model'), parts along dimension 0, may hold values from -0.25 to 0.25
- master_up: float32 [4096, 3072], P(('shift', 'replica'), 'model'), parts along dimension 0, may hold values from -0.25 to 0.25
- master_down: float32 [12288, 1024], P(('shift', 'model'), 'replica'), parts along dimension 0, may hold values from -0.15625 to 0.15625
- master_norm: float32 [4096], P(('shift', 'replica')), parts along dimension 0, may hold values from 0.25 to 1.75
- memory_gate: float32 [4096, 3072], P(('shift', 'replica'), 'model'), parts along dimension 0, may hold values from -0.1875 to 0.1875
- memory_up: float32 [4096, 3072], P(('shift', 'replica'), 'model'), parts along dimension 0, may hold values from -0.1875 to 0.1875
- memory_down: float32 [12288, 1024], P(('shift', 'model'), 'replica'), parts along dimension 0, may hold values from -0.109375 to 0.109375
- memory_norm: float32 [4096], P(('shift', 'replica')), parts along dimension 0, may hold values from -1.75 to 1.75
Outputs:
- compute_gate: bfloat16 [4096, 3072], P('shift', 'model'), parts along dimension 0
- compute_up: bfloat16 [4096, 3072], P('shift', 'model'), parts along dimension 0
- compute_down: bfloat16 [12288, 1024], P(('shift', 'model')), parts along dimension 0
- compute_norm: bfloat16 [4096], P('shift'), parts along dimension 0
- stepped_gate: float32 [4096, 3072], P(('shift', 'replica'), 'model'), parts along dimension 0
- stepped_up: float32 [4096, 3072], P(('shift', 'replica'), 'model'), parts along dimension 0
- stepped_down: float32 [12288, 1024], P(('shift', 'model'), 'replica'), parts along dimension 0
- stepped_norm: float32 [4096], P(('shift', 'replica')), parts along dimension 0
- state_new_gate: float32 [4096, 3072], P(('shift', 'replica'), 'model'), parts along dimension 0
- state_new_up: float32 [4096, 3072], P(('shift', 'replica'), 'model'), parts along dimension 0
- state_new_down: float32 [12288, 1024], P(('shift', 'model'), 'replica'), parts along dimension 0
- state_new_norm: float32 [4096], P(('shift', 'replica')), parts along dimension 0
There are 4 independent parts, one for each index of `shift`. A program takes and returns all parts, laid end to end along the dimension named above; each array names one. Nothing has to cross between parts.
All inputs are finite; a program needn't handle non-finite values.
Results may differ from a plain program's by a relative error of at most 0.001.
Values may be sent and summed in bfloat16 or wider, within the bound.
A program may use at most 128 MiB of HBM per device.

v0:
```python
import jax
import jax.numpy as jnp
from jax import lax
from jax.sharding import PartitionSpec as P

learn_rate = 0.5
hold_rate = 0.9


def split_up(array, dim, devices):
    before, after = (array.shape[:dim], array.shape[dim + 1 :])
    return jnp.moveaxis(array.reshape(*before, devices, -1, *after), dim, 0)


def sum_together(arrays, axis, dims):
    devices = lax.axis_size(axis)
    blocks = [split_up(a, dim, devices) for a, dim in zip(arrays, dims)]
    lines = jnp.concatenate([b.reshape(devices, -1) for b in blocks], axis=1)
    width = max(16, -(-lines.shape[1] // 1024) * 8)
    lines = jnp.pad(lines, ((0, 0), (0, width * 128 - lines.shape[1]))).reshape(-1, 128)
    line, at, outs = (lax.psum_scatter(lines, axis, tiled=True).reshape(-1), 0, [])
    for b in blocks:
        part = b[0]
        outs.append(line[at : at + part.size].reshape(part.shape))
        at += part.size
    return tuple(outs)


def from_everyone(array, axis):
    copies = jnp.broadcast_to(array, (lax.axis_size(axis), *array.shape))
    return lax.all_to_all(copies, axis, split_axis=0, concat_axis=0, tiled=True)


def of_everyone(array, axis):
    return from_everyone(array, axis).sum(axis=0)


def in_one(arrays, axis):
    ends = [0]
    for a in arrays:
        ends.append(ends[-1] + a.size)
    running = of_everyone(jnp.concatenate([a.ravel() for a in arrays]), axis)
    return tuple((running[b:e].reshape(a.shape) for a, b, e in zip(arrays, ends, ends[1:])))


def rows_first(arrays, axis, dims):
    turned = [jnp.moveaxis(a, dim, 0) for a, dim in zip(arrays, dims)]
    both = jnp.concatenate([t.reshape(len(t), -1) for t in turned], axis=1)
    filled, at, outs = (lax.all_gather(both, axis, axis=0, tiled=True), 0, [])
    for t, dim in zip(turned, dims):
        section = filled[:, at : at + t[0].size].reshape(-1, *t.shape[1:])
        outs.append(jnp.moveaxis(section, 0, dim))
        at += t[0].size
    return tuple(outs)


def on_device(
    partial_gate,
    partial_up,
    partial_down,
    partial_norm,
    master_gate,
    master_up,
    master_down,
    master_norm,
    memory_gate,
    memory_up,
    memory_down,
    memory_norm,
):
    mean_gate, mean_up, mean_down = sum_together(
        (partial_gate[0], partial_up[0], partial_down[0]), "replica", (0, 0, 1)
    )
    whole_norm = of_everyone(partial_norm[0], "replica")
    place = lax.axis_index("replica")
    mean_norm = lax.dynamic_slice_in_dim(
        whole_norm, place * master_norm.shape[0], master_norm.shape[0]
    )
    mean_rate = lax.axis_size("replica") ** (-0.5)
    mean_gate = mean_gate * mean_rate
    mean_up = mean_up * mean_rate
    mean_down = mean_down * mean_rate
    mean_norm = mean_norm * mean_rate
    own_gate, own_up, own_down, slope_gate_norm, slope_up_norm, slope_down_norm = in_one(
        (
            jnp.sum(master_gate * master_gate, axis=1, keepdims=True),
            jnp.sum(master_up * master_up, axis=1, keepdims=True),
            jnp.sum(master_down * master_down, axis=0, keepdims=True),
            jnp.sum(mean_gate * mean_gate, axis=1, keepdims=True),
            jnp.sum(mean_up * mean_up, axis=1, keepdims=True),
            jnp.sum(mean_down * mean_down, axis=0, keepdims=True),
        ),
        "model",
    )
    mean_gate = mean_gate * (jnp.sqrt(own_gate) * lax.rsqrt(slope_gate_norm + 1e-06))
    mean_up = mean_up * (jnp.sqrt(own_up) * lax.rsqrt(slope_up_norm + 1e-06))
    mean_down = mean_down * (jnp.sqrt(own_down) * lax.rsqrt(slope_down_norm + 1e-06))
    state_new_gate = hold_rate * memory_gate + mean_gate
    stepped_gate = master_gate - learn_rate * state_new_gate
    state_new_up = hold_rate * memory_up + mean_up
    stepped_up = master_up - learn_rate * state_new_up
    state_new_down = hold_rate * memory_down + mean_down
    stepped_down = master_down - learn_rate * state_new_down
    state_new_norm = hold_rate * memory_norm + mean_norm
    stepped_norm = master_norm - learn_rate * state_new_norm
    compute_gate, compute_up, compute_down, compute_norm = rows_first(
        (
            stepped_gate.astype(jnp.bfloat16),
            stepped_up.astype(jnp.bfloat16),
            stepped_down.astype(jnp.bfloat16),
            stepped_norm.astype(jnp.bfloat16),
        ),
        "replica",
        (0, 0, 1, 0),
    )
    return (
        compute_gate,
        compute_up,
        compute_down,
        compute_norm,
        stepped_gate,
        stepped_up,
        stepped_down,
        stepped_norm,
        state_new_gate,
        state_new_up,
        state_new_down,
        state_new_norm,
    )


def solution(mesh):
    return jax.shard_map(
        on_device,
        mesh=mesh,
        in_specs=(
            P(("shift", "replica"), None, "model"),
            P(("shift", "replica"), None, "model"),
            P(("shift", "replica"), "model", None),
            P(("shift", "replica"), None),
            P(("shift", "replica"), "model"),
            P(("shift", "replica"), "model"),
            P(("shift", "model"), "replica"),
            P(("shift", "replica")),
            P(("shift", "replica"), "model"),
            P(("shift", "replica"), "model"),
            P(("shift", "model"), "replica"),
            P(("shift", "replica")),
        ),
        out_specs=(
            P("shift", "model"),
            P("shift", "model"),
            P(("shift", "model"), None),
            P("shift"),
            P(("shift", "replica"), "model"),
            P(("shift", "replica"), "model"),
            P(("shift", "model"), "replica"),
            P(("shift", "replica")),
            P(("shift", "replica"), "model"),
            P(("shift", "replica"), "model"),
            P(("shift", "model"), "replica"),
            P(("shift", "replica")),
        ),
        check_vma=False,
    )
```

profile of v0, /device:TPU:1, one launch (start us, length us, event | category | flops | bytes accessed | tf_op | source)
XLA Modules:
  0.0 188.4 jit_solution(4625872434043212699)
XLA Ops:
  7.2 0.0 reduce-scatter.2.cloned.1.call-start
  7.2 2.4 %copy.52 = f32[1,768,1024]{1,2,0:T(8,128)S(1)} copy(f32[1,768,1024]{2,1,0:T(8,128)} %param.14) | data formatting | bytes 6291456 | tf_op args[2]
  9.6 4.1 %copy.53 = f32[16,768,64]{2,1,0:T(8,128)} copy(f32[16,768,64]{1,2,0:T(8,128)S(1)} %bitcast.10) | data formatting | bytes 6291456 | tf_op jit(solution)/shard_map/transpose | solution.py:12
  13.7 4.9 %reshape.85 = f32[16,49152]{1,0:T(8,128)} reshape(f32[16,768,64]{2,1,0:T(8,128)} %copy.53) | data formatting | bytes 6291456 | tf_op jit(solution)/shard_map/reshape | solution.py:18
  18.6 2.2 %reshape_reshape_squeeze.6 = f32[16,49152]{1,0:T(8,128)S(1)} reshape(f32[1,1024,768]{2,1,0:T(8,128)} %param.12) | data formatting | bytes 6291456 | tf_op jit(solution)/shard_map/reshape;reshape;squeeze | solution.py:18
  20.8 3.4 %reshape_reshape_squeeze.7 = f32[16,49152]{1,0:T(8,128)} reshape(f32[1,1024,768]{2,1,0:T(8,128)} %param.13) | data formatting | bytes 6291456 | tf_op jit(solution)/shard_map/reshape;reshape;squeeze | solution.py:18
  24.2 6.2 %pad_maximum_fusion = f32[16,147456]{1,0:T(8,128)} fusion(f32[16,49152]{1,0:T(8,128)} %reshape.85, f32[16,49152]{1,0:T(8,128)} %reshape_reshape_squeeze.7, f32[16,49152]{1,0:T(8,128)S(1)} %reshape_reshape_squeeze.6), kind=kLoop, calls=%fused_computation | loop fusion | flops 4718592 | bytes 18874368 | tf_op jit(solution)/shard_map/concatenate | solution.py:18
  30.4 10.4 %reshape.86 = f32[18432,128]{1,0:T(8,128)} reshape(f32[16,147456]{1,0:T(8,128)} %pad_maximum_fusion) | data formatting | bytes 18874368 | tf_op jit(solution)/shard_map/reshape | solution.py:20
  40.9 0.0 copy-start.6
  40.9 0.0 copy-start.1
  40.9 0.0 copy-start.2
  40.9 0.0 copy-start
  40.9 0.0 reduce-scatter.2.cloned.1.call-update
  40.9 0.0 copy-start.7
  40.9 0.0 copy-start.8
  40.9 0.0 copy-start.3
  40.9 0.0 copy-start.4
  40.9 0.6 copy-done.6
  41.5 0.7 broadcast_in_dim.7
  42.2 10.0 %all-to-all-start.1 = ((f32[16,1,1024]{2,1,0:T(1,128)}), f32[16,1,1024]{2,1,0:T(1,128)S(1)}, u32[]{:S(2)}, u32[]{:S(2)}) async-start(f32[16,1,1024]{2,1,0:T(1,128)} %broadcast_in_dim.7), calls=%async_computation.2 | async-start | bytes 131072 | tf_op jit(solution)/shard_map/all_to_all | solution.py:31
  52.2 0.0 copy-done.1
  52.2 0.0 copy-done.2
  52.2 0.1 multiply_reduce_fusion.4
  52.3 0.0 copy-start.5
  52.3 0.0 copy-done
  52.3 0.1 multiply_reduce_fusion.3
  52.5 7.6 %all-to-all-done.1 = f32[16,1,1024]{2,1,0:T(1,128)S(1)} async-done(((f32[16,1,1024]{2,1,0:T(1,128)}), f32[16,1,1024]{2,1,0:T(1,128)S(1)}, u32[]{:S(2)}, u32[]{:S(2)}) %all-to-all-start.1) | async-done | bytes 65568 | tf_op jit(solution)/shard_map/all_to_all | solution.py:31
  60.0 0.1 reduce_sum.97
  60.1 54.7 %reduce-scatter.2.cloned.1.call-done = f32[1152,128]{1,0:T(8,128)} async-done(((f32[18432,128]{1,0:T(8,128)}), f32[1152,128]{1,0:T(8,128)}) %reduce-scatter.2.cloned.1.call-update) | async-done | bytes 589840 | tf_op jit(solution)/shard_map/reduce_scatter | solution.py:21
  114.8 1.3 multiply_reduce_fusion.1
  116.1 0.1 reshape.88
  116.3 0.1 multiply_reduce_fusion
  116.4 0.1 reduce_sum.90
  116.5 0.1 reduce_sum.91
  116.6 0.1 reduce_sum.93
  116.8 0.1 reduce_sum.94
  116.9 0.1 concatenate.10
  117.0 0.6 broadcast_in_dim.6
  117.6 4.0 %all-to-all-start = ((f32[4,1,384]{2,1,0:T(1,128)}), f32[4,1,384]{2,1,0:T(1,128)S(1)}, u32[]{:S(2)}, u32[]{:S(2)}) async-start(f32[4,1,384]{2,1,0:T(1,128)} %broadcast_in_dim.6), calls=%async_computation.1 | async-start | bytes 12288 | tf_op jit(solution)/shard_map/all_to_all | solution.py:31
  121.6 0.0 all-gather.2.cloned.1.call-start
  121.6 0.0 copy-done.7
  121.6 0.0 copy-done.8
  121.6 0.6 convert_bitcast_fusion.1
  122.2 0.1 copy.57
  122.3 0.1 copy.55
  122.6 3.2 %all-to-all-done = f32[4,1,384]{2,1,0:T(1,128)S(1)} async-done(((f32[4,1,384]{2,1,0:T(1,128)}), f32[4,1,384]{2,1,0:T(1,128)S(1)}, u32[]{:S(2)}, u32[]{:S(2)}) %all-to-all-start) | async-done | bytes 6176 | tf_op jit(solution)/shard_map/all_to_all | solution.py:31
  125.8 0.1 multiply_multiply_fusion.2
  125.9 0.0 copy-done.3
  125.9 0.8 convert_bitcast_fusion
  126.7 0.0 copy-done.4
  126.7 0.8 fusion
  127.5 0.0 copy-done.5
  127.6 0.8 fusion.1
  128.4 0.7 pad_maximum_fusion.1
  129.1 0.0 all-gather.2.cloned.1.call-update
  129.2 44.7 %all-gather.2.cloned.1.call-done = bf16[1024,2305]{1,0:T(8,128)(2,1)} async-done(((bf16[64,2305]{1,0:T(8,128)(2,1)}), bf16[1024,2305]{1,0:T(8,128)(2,1)}) %all-gather.2.cloned.1.call-update) | async-done | bytes 4720656 | tf_op jit(solution)/shard_map/all_gather | solution.py:49
  173.9 4.3 %slice_bitcast_fusion = (bf16[768,1024]{0,1:T(8,128)(2,1)S(1)}, bf16[1024,768]{1,0:T(8,128)(2,1)}, bf16[1024,768]{1,0:T(8,128)(2,1)}) fusion(bf16[1024,2305]{1,0:T(8,128)(2,1)} %all-gather.2.cloned.1.call-done), kind=kLoop, calls=%fused_computation.1 | loop fusion | bytes 9437184 | tf_op jit(solution)/shard_map/transpose | solution.py:52
  178.2 1.6 copy.58
  179.8 1.7 slice_reduce_fusion
  (3 shorter events, 0.1 us)
Async XLA Ops:
  7.2 107.7 %reduce-scatter.2.cloned.1.call-start = ((), (), s32[]{:S(2)}) async-start(), calls=%async_computation.3 | async-start | bytes 10027008 | tf_op jit(solution)/shard_map/reduce_scatter | solution.py:21
  40.9 0.7 copy-start.6
  40.9 11.3 %copy-start.1 = (f32[64,768]{1,0:T(8,128)S(1)}, f32[64,768]{1,0:T(8,128)}, u32[]{:S(2)}) copy-start(f32[64,768]{1,0:T(8,128)} %param.16) | copy-start | bytes 589828
  40.9 11.3 %copy-start.2 = (f32[64,768]{1,0:T(8,128)S(1)}, f32[64,768]{1,0:T(8,128)}, u32[]{:S(2)}) copy-start(f32[64,768]{1,0:T(8,128)} %param.17) | copy-start | bytes 589828
  40.9 11.5 %copy-start = (f32[768,64]{0,1:T(8,128)S(1)}, f32[768,64]{0,1:T(8,128)}, u32[]{:S(2)}) copy-start(f32[768,64]{0,1:T(8,128)} %param.18) | copy-start | bytes 589828
  40.9 80.7 %copy-start.7 = (f32[64]{0:T(128)S(1)}, f32[64]{0:T(128)}, u32[]{:S(2)}) copy-start(f32[64]{0:T(128)} %param.19) | copy-start | bytes 772
  40.9 80.7 %copy-start.8 = (f32[64]{0:T(128)S(1)}, f32[64]{0:T(128)}, u32[]{:S(2)}) copy-start(f32[64]{0:T(128)} %param.23) | copy-start | bytes 772
  40.9 84.9 %copy-start.3 = (f32[768,64]{0,1:T(8,128)S(1)}, f32[768,64]{0,1:T(8,128)}, u32[]{:S(2)}) copy-start(f32[768,64]{0,1:T(8,128)} %param.22) | copy-start | bytes 589828
  40.9 85.8 %copy-start.4 = (f32[64,768]{1,0:T(8,128)S(1)}, f32[64,768]{1,0:T(8,128)}, u32[]{:S(2)}) copy-start(f32[64,768]{1,0:T(8,128)} %param.20) | copy-start | bytes 589828
  42.2 17.8 %all-to-all-start.1 = ((f32[16,1,1024]{2,1,0:T(1,128)}), f32[16,1,1024]{2,1,0:T(1,128)S(1)}, u32[]{:S(2)}, u32[]{:S(2)}) async-start(f32[16,1,1024]{2,1,0:T(1,128)} %broadcast_in_dim.7), calls=%async_computation.2 | async-start | bytes 131072 | tf_op jit(solution)/shard_map/all_to_all | solution.py:31
  52.3 75.2 %copy-start.5 = (f32[64,768]{1,0:T(8,128)S(1)}, f32[64,768]{1,0:T(8,128)}, u32[]{:S(2)}) copy-start(f32[64,768]{1,0:T(8,128)} %param.21) | copy-start | bytes 589828
  117.6 8.1 %all-to-all-start = ((f32[4,1,384]{2,1,0:T(1,128)}), f32[4,1,384]{2,1,0:T(1,128)S(1)}, u32[]{:S(2)}, u32[]{:S(2)}) async-start(f32[4,1,384]{2,1,0:T(1,128)} %broadcast_in_dim.6), calls=%async_computation.1 | async-start | bytes 12288 | tf_op jit(solution)/shard_map/all_to_all | solution.py:31
  121.6 52.3 %all-gather.2.cloned.1.call-start = ((), (), s32[]{:S(2)}) async-start(), calls=%async_computation.4 | async-start | bytes 5292032 | tf_op jit(solution)/shard_map/all_gather | solution.py:49
Sparse Core Ops, SparseCore 0:
  41.0 73.7 reduce-scatter.1
  129.3 44.5 all-gather.1
where the time goes:
time: 189 us; the launch traced here: 188 us
  waiting for transfers between devices  110 us (58%)
  local copies, waits for them, and re-layouts  37.7 us (20%)
  between operations  14.2 us (8%)
  starting transfers between devices  14 us (7%)
  other arithmetic  12.1 us (6%)
    reduce_scatter x1, waiting for transfers between devices, sum_together(): lax.psum_scatter(lines, axis, tiled=True).reshape(-1)  54.7 us
    all_gather x1, waiting for transfers between devices, rows_first(): filled, at, outs = (lax.all_gather(both, axis, axis=0, tiled=True), 0, [])  44.7 us
    all_to_all x2, starting transfers between devices, from_everyone(): return lax.all_to_all(copies, axis, split_axis=0, concat_axis=0, tiled=True)  14 us
    all_to_all x2, waiting for transfers between devices, from_everyone(): return lax.all_to_all(copies, axis, split_axis=0, concat_axis=0, tiled=True)  10.8 us
    reshape x1, local copies, waits for them, and re-layouts, sum_together(): jnp.pad(lines, ((0, 0), (0, width * 128 - lines.shape[1]))).reshape(-1, 128)  10.4 us
    concatenate x1, other arithmetic, sum_together(): lines = jnp.concatenate([b.reshape(devices, -1) for b in blocks], axis=1)  6.23 us
    another operation x2, local copies, waits for them, and re-layouts, sum_together(): lines = jnp.concatenate([b.reshape(devices, -1) for b in blocks], axis=1)  5.54 us
    reshape x1, local copies, waits for them, and re-layouts, sum_together(): lines = jnp.concatenate([b.reshape(devices, -1) for b in blocks], axis=1)  4.93 us
  transfers between devices with their start and end apart: 4, of which 4 were waited for; matrix products, arithmetic and copies ran while one was open for 1% of the time, Pallas kernels for 0%

commit v1 on v0

v1 whole, which is shorter than its diff:
```python
import functools

import jax
import jax.numpy as jnp
from jax import lax
from jax.experimental import pallas as pl
from jax.experimental.pallas import tpu as pltpu
from jax.sharding import PartitionSpec as P

MESH = pl.DeviceIdType.MESH
F32, BF16 = jnp.float32, jnp.bfloat16
learn_rate = 0.5
hold_rate = 0.9

Z = 8
X = 4
ROWS = 64
COLS = 768
HALF = 384
STEP = (1, -1)
LONG = ((3, 4), (4, 3))
SCALE = 8192.0


def encode(v):
    v = v * SCALE
    a = v * v
    a = a * a
    a = a * a
    return jnp.where(v < 0, -a, a).astype(BF16)


def decode(y):
    y = y.astype(F32)
    a = jnp.abs(y)
    q = lax.rsqrt(lax.rsqrt(jnp.maximum(a, 1e-37)))
    x = q * lax.rsqrt(q) * (1.0 / SCALE)
    x = jnp.where(a < 2e-37, 0.0, x)
    return jnp.where(y < 0, -x, x)


def plan():
    wire, lag = 1.06, 2.2
    tasks = {}
    for t in range(3):
        for d in range(2):
            for h in range(2):
                top = LONG[d][h]
                for k in range(top, 0, -1):
                    needs = [("got", "rs", t, d, h, k + 1)] if k < top else []
                    needs.append(("in", t, STEP[d] * k % Z))
                    tasks["rs", t, d, h, k] = (needs, 0.3 if k < top else 0.2, d, 100 + 10 * k - 3 * t)
                for k in range(1, top + 1):
                    needs = [("did", "update", t)] if k == 1 else []
                    if k > 1:
                        needs = [("got", "ag", t, d, h, k - 1)]
                    tasks["ag", t, d, h, k] = (needs, 0.05, d, 50 - 5 * k - t)
                tasks["ag", t, d, h, top + 1] = ([("got", "ag", t, d, h, top)], 0.05, None, 10)
        ends = [("got", "rs", t, d, h, 1) for d in range(2) for h in range(2)]
        tasks["sum", t] = (ends + [("in", t, 0)], 0.5, None, 200)
        tasks["master", t] = ([("late", 8.0 + t)], 0.3, None, 60)
        tasks["update", t] = ([("after", "sum", t, 3.0), ("did", "master", t)], 0.6, None, 190)
    tasks["norm_out",] = ([("did", "sum", 0)], 0.1, None, 55)
    tasks["norm_in",] = ([("after", "norm_out", 8.0)], 0.3, None, 54)
    order, now, free, arrive, done = [], 2.5, [0.0, 0.0], {}, {}

    def ready(needs):
        at = 0.0
        for n in needs:
            if n[0] == "got":
                at = max(at, arrive.get(n[1:], 1e9))
            elif n[0] == "in":
                off = (4, 3, 5, 2, 6, 1, 7, 0).index(n[2])
                at = max(at, 3.0 + 0.32 * (off * 3 + n[1] + 1))
            elif n[0] == "did":
                at = max(at, done.get(n[1:], 1e9))
            elif n[0] == "late":
                at = max(at, n[1])
            else:
                at = max(at, done.get(n[1:-1], 1e9) + n[-1])
        return at

    while tasks:
        times = {k: ready(v[0]) for k, v in tasks.items()}
        open_ = [k for k in tasks if times[k] <= now]
        if not open_:
            now = min(times.values())
            continue
        pick = max(open_, key=lambda k: (tasks[k][3], k))
        _, cost, link, _ = tasks.pop(pick)
        now += cost
        done[pick] = now
        order.append(pick)
        if link is not None:
            free[link] = max(free[link], now) + wire
            arrive[pick] = free[link] + lag
    return order, now


def kernel(*refs):
    it = iter(refs)
    take = lambda n: [next(it) for _ in range(n)]
    pg, pu, pd, pk, mg, mu, md, eg, eu, ed = take(10)
    cg, cu, cd, cn, sg, su, sd, tg, tu, td, own_n = take(11)
    own_gu, peer_gu, own_d, peer_d = take(4)
    rs_out_gu, rs_in_gu, rs_out_d, rs_in_d = take(4)
    ag_gu, ag_d = take(2)
    mean_gu, mean_d = take(2)
    mas_gu, mem_gu, mas_d, mem_d, mas_half, mem_half = take(6)
    new_gu, new_d, give_d = take(3)
    sq_gu, sq_d = take(2)
    packet, packets, norm_mas, norm_mem, cn_v, own_v = take(6)
    (load_sem, swap_s, swap_r, rs_s, rs_r, ag_s, ag_r, agp_s, agp_r, out_sem, mast_sem, half_s, half_r,
     sq_s, sq_r, pk_sem, pk_s, pk_r, new_sem, give_s, give_r, norm_sem) = take(22)

    r = lax.axis_index("replica")
    z, c = r // 2, r % 2
    peer = r + 1 - 2 * c
    x = lax.axis_index("model")
    chip = lambda off: lax.rem(z + off + 2 * Z, Z)
    beside = lambda d: {"replica": 2 * chip(STEP[d]) + c}
    across = lambda i: lax.rem(x + i, X)

    def remote(src, dst, s, rv, dev):
        return pltpu.make_async_remote_copy(src_ref=src, dst_ref=dst, send_sem=s, recv_sem=rv, device_id=dev, device_id_type=MESH)

    pending = []

    def go(copy):
        copy.start()
        pending.append(copy)
        return copy

    parts = (pg, pu, pd)

    def block(t, at, core):
        if t < 2:
            return parts[t].at[at, core]
        return pd.at[pl.ds(pl.multiple_of(HALF * core, HALF), HALF), pl.ds(pl.multiple_of(128 * at, 128), 128)]

    own_at = lambda t, at: own_gu.at[t, at] if t < 2 else own_d.at[at]
    peer_at = lambda t, at: peer_gu.at[t, at] if t < 2 else peer_d.at[at]
    offs = (4, 3, 5, 2, 6, 1, 7, 0)
    loads, swaps = {}, {}
    for off in offs:
        for t in range(3):
            at = chip(off)
            loads[t, off] = pltpu.make_async_copy(block(t, at, c), own_at(t, at), load_sem.at[t, off])
            loads[t, off].start()

    barrier = pltpu.get_barrier_semaphore()
    hello = [{"replica": peer}, beside(0), beside(1)]
    for i in range(1, X):
        hello.append({"model": across(i)})
        hello.append({"replica": peer, "model": across(i)})
    for dev in hello:
        pl.semaphore_signal(barrier, inc=1, device_id=dev, device_id_type=MESH)
    pl.semaphore_wait(barrier, len(hello))

    for off in offs:
        for t in range(3):
            at = chip(off)
            swaps[t, off] = remote(block(t, at, 1 - c), peer_at(t, at), swap_s.at[t, off], swap_r.at[t, off], {"replica": peer})
            swaps[t, off].start()

    masters = {}
    for t, (m, e) in enumerate(((mg, eg), (mu, eu), (md, ed))):
        for i, (ref, gu, dn) in enumerate(((m, mas_gu, mas_d), (e, mem_gu, mem_d))):
            masters[t, i] = pltpu.make_async_copy(ref, gu.at[t] if t < 2 else dn, mast_sem.at[t, i])
            masters[t, i].start()
    halves = []
    for i, (ref, buf) in enumerate(((md, mas_half), (ed, mem_half))):
        rows = pl.ds(pl.multiple_of(HALF * (1 - c), HALF), HALF)
        halves.append(remote(ref.at[rows], buf, half_s.at[i], half_r.at[i], {"replica": peer}))
        halves[-1].start()
    load_packet = pltpu.make_async_copy(pk, packet, pk_sem)
    load_packet.start()

    have = set()

    def need(t, off):
        if (t, off) not in have:
            have.add((t, off))
            loads[t, off].wait()
            swaps[t, off].wait_recv()
            pending_sends.append(swaps[t, off])

    pending_sends = []

    rs_out = lambda t, d, h, k: rs_out_gu.at[t, d, h, k - 1] if t < 2 else rs_out_d.at[d, h, k - 1]
    rs_in = lambda t, d, h, k: rs_in_gu.at[t, d, h, k - 1] if t < 2 else rs_in_d.at[d, h, k - 1]

    def rs_copy(t, d, h, k):
        return remote(rs_out(t, d, h, k), rs_in(t, d, h, k), rs_s.at[t, d, h, k - 1], rs_r.at[t, d, h, k - 1], beside(d))

    size = lambda t: 16 if t < 2 else 96

    def rs_send(t, d, h, k):
        off = STEP[d] * k % Z
        need(t, off)
        at, n = chip(off), size(t)
        chained = k < LONG[d][h]
        if chained:
            rs_copy(t, d, h, k + 1).wait_recv()
        own, other, out = own_at(t, at), peer_at(t, at), rs_out(t, d, h, k)
        arrived = rs_in(t, d, h, k + 1) if chained else None

        def body(i, _):
            here = pl.ds(pl.multiple_of(i * n, n), n)
            there = pl.ds(pl.multiple_of(2 * n * h + i * n, n), n)
            v = own[there, :] + other[there, :]
            if chained:
                v = v + decode(arrived[here, :])
            out[here, :] = encode(v)
            return 0

        lax.fori_loop(0, 2, body, 0)
        copy = rs_copy(t, d, h, k)
        copy.start()
        pending_sends.append(copy)

    def sq_slot(w, t):
        return sq_gu.at[w, t, x] if t < 2 else sq_d.at[w, 2 * x + c]

    def sq_copies(w, t):
        out = []
        for i in range(1, X):
            out.append(remote(sq_slot(w, t), sq_slot(w, t), sq_s.at[w, t, i], sq_r.at[w, t, i], {"model": across(i)}))
        if t == 2:
            for i in range(X):
                out.append(remote(sq_slot(w, t), sq_slot(w, t), sq_s.at[w, t, X + i], sq_r.at[w, t, X + i],
                                  {"replica": peer, "model": across(i)}))
        return out

    def share(w, t):
        for copy in sq_copies(w, t):
            copy.start()
            pending_sends.append(copy)

    def shared(w, t):
        for copy in sq_copies(w, t):
            copy.wait_recv()

    def lanes(v):
        total = v[:, :128]
        for j in range(1, v.shape[1] // 128):
            total = total + v[:, 128 * j : 128 * (j + 1)]
        return total

    def eights(v):
        total = v[:8]
        for j in range(1, v.shape[0] // 8):
            total = total + v[8 * j : 8 * (j + 1)]
        return total

    def sum_up(t):
        need(t, 0)
        for d in range(2):
            for h in range(2):
                rs_copy(t, d, h, 1).wait_recv()
        n = size(t)
        own, other = own_at(t, z), peer_at(t, z)
        for h in range(2):
            ahead, back = rs_in(t, 0, h, 1), rs_in(t, 1, h, 1)

            def body(i, carry):
                here = pl.ds(pl.multiple_of(i * n, n), n)
                there = pl.ds(pl.multiple_of(2 * n * h + i * n, n), n)
                v = (own[there, :] + other[there, :]) + (decode(ahead[here, :]) + decode(back[here, :]))
                v = v * (2 * Z) ** -0.5
                if t < 2:
                    mean_gu[t, there, :] = v
                    sq_gu[0, t, x, there, :] = lanes(v * v)
                    return carry
                mean_d[there, :] = v
                return carry + eights(v * v)

            first = jnp.zeros((8, 128), F32) if h == 0 else total
            total = lax.fori_loop(0, 2, body, first)
        if t == 2:
            sq_d[0, 2 * x + c] = total
        share(0, t)

    lane = lax.broadcasted_iota(jnp.int32, (96, 128), 1)
    mine = lax.broadcast_in_dim(c, (96, 128), ()) == jnp.where(lane < 64, 0, 1)

    def join(own, other):
        a = jnp.concatenate([own, own], axis=1)
        b = jnp.concatenate([other, other], axis=1)
        return jnp.where(mine, a, b)

    def master(t):
        masters[t, 0].wait()
        masters[t, 1].wait()
        n = size(t)
        if t == 2:
            halves[0].wait_recv()
            halves[1].wait_recv()
            pending_sends.extend(halves)

        def body(i, carry):
            here = pl.ds(pl.multiple_of(i * n, n), n)
            if t < 2:
                v = mas_gu[t, here, :]
                sq_gu[1, t, x, here, :] = lanes(v * v)
                return carry
            there = pl.ds(pl.multiple_of(HALF * c + i * n, n), n)
            v = join(mas_d[there, :], mas_half[here, :])
            return carry + eights(v * v)

        total = lax.fori_loop(0, 4, body, jnp.zeros((8, 128), F32))
        if t == 2:
            sq_d[1, 2 * x + c] = total
        share(1, t)

    def update(t):
        shared(0, t)
        shared(1, t)
        n = size(t)
        if t == 2:
            def ratio_of(w):
                total = sq_d[w, 0]
                for j in range(1, 2 * X):
                    total = total + sq_d[w, j]
                return jnp.sum(total, axis=0, keepdims=True)
            ratio_d = jnp.sqrt(ratio_of(1)) * lax.rsqrt(ratio_of(0) + 1e-6)

        def body(i, _):
            here = pl.ds(pl.multiple_of(i * n, n), n)
            if t < 2:
                def whole(w):
                    total = sq_gu[w, t, 0, here, :]
                    for j in range(1, X):
                        total = total + sq_gu[w, t, j, here, :]
                    return jnp.sum(total, axis=1, keepdims=True)
                ratio = jnp.sqrt(whole(1)) * lax.rsqrt(whole(0) + 1e-6)
                state = hold_rate * mem_gu[t, here, :] + mean_gu[t, here, :] * ratio
                stepped = mas_gu[t, here, :] - learn_rate * state
                new_gu[t, 0, here, :] = stepped
                new_gu[t, 1, here, :] = state
                ag_gu[t, z, here, :] = stepped.astype(BF16)
                return 0
            there = pl.ds(pl.multiple_of(HALF * c + i * n, n), n)
            state = hold_rate * join(mem_d[there, :], mem_half[here, :]) + mean_d[here, :] * ratio_d
            stepped = join(mas_d[there, :], mas_half[here, :]) - learn_rate * state
            ag_d[z, here, :] = stepped.astype(BF16)
            for j, v in enumerate((stepped, state)):
                turned = jnp.concatenate([v[:, 64:], v[:, :64]], axis=1)
                new_d[j, here, :] = jnp.where(mine[:, :64], v[:, :64], turned[:, :64])
                give_d[j, here, :] = jnp.where(mine[:, :64], turned[:, :64], v[:, :64])
            return 0

        lax.fori_loop(0, 4, body, 0)
        if t < 2:
            for j, ref in enumerate(((sg, su)[t], (tg, tu)[t])):
                go(pltpu.make_async_copy(new_gu.at[t, j], ref, new_sem.at[t, j]))
        else:
            rows = pl.ds(pl.multiple_of(HALF * c, HALF), HALF)
            for j, ref in enumerate((sd, td)):
                go(pltpu.make_async_copy(new_d.at[j], ref.at[rows], new_sem.at[t, j]))
                gift = remote(give_d.at[j], ref.at[rows], give_s.at[j], give_r.at[j], {"replica": peer})
                gift.start()
                gifts.append(gift)
        for h in range(2):
            deliver(t, 0, h)

    gifts = []
    ag_at = lambda t, at, h: ag_gu.at[t, at, pl.ds(32 * h, 32)] if t < 2 else ag_d.at[at, pl.ds(192 * h, 192)]

    def place(t, at, h, core):
        if t < 2:
            return (cg, cu)[t].at[at, core, pl.ds(32 * h, 32)]
        return cd.at[pl.ds(pl.multiple_of(HALF * core + 192 * h, 192), 192), pl.ds(pl.multiple_of(128 * at, 128), 128)]

    delivered = []

    def deliver(t, off, h):
        at = chip(off)
        go(pltpu.make_async_copy(ag_at(t, at, h), place(t, at, h, c), out_sem.at[t, off % Z, h]))
        copy = remote(ag_at(t, at, h), place(t, at, h, c), agp_s.at[t, off % Z, h], agp_r.at[t, off % Z, h], {"replica": peer})
        copy.start()
        delivered.append(copy)

    def ag_copy(t, d, h, k, from_here):
        at = chip(-STEP[d] * (k - 1)) if from_here else chip(-STEP[d] * k)
        return remote(ag_at(t, at, h), ag_at(t, at, h), ag_s.at[t, d, h, k - 1], ag_r.at[t, d, h, k - 1], beside(d))

    def ag_step(t, d, h, k):
        if k > 1:
            ag_copy(t, d, h, k - 1, False).wait_recv()
        if k <= LONG[d][h]:
            copy = ag_copy(t, d, h, k, True)
            copy.start()
            pending_sends.append(copy)
        if k > 1:
            deliver(t, -STEP[d] * (k - 1), h)

    def norm_copies():
        return [remote(packet, packets.at[r], pk_s.at[j], pk_r.at[j], {"replica": lax.rem(r + j, 2 * Z)}) for j in range(1, 2 * Z)]

    def norm_out():
        load_packet.wait()
        for copy in norm_copies():
            copy.start()
            pending_sends.append(copy)

    def norm_in():
        packets[r] = packet[...]
        for copy in norm_copies():
            copy.wait_recv()
        total = packets[0, :8, :]
        for j in range(1, 2 * Z):
            total = total + packets[j, :8, :]
        mean = total * (2 * Z) ** -0.5
        low = lax.broadcasted_iota(jnp.int32, (1, 128), 1) < 64
        turn = lambda v: jnp.concatenate([v[:, 64:], v[:, :64]], axis=1)
        for j in range(Z):
            a, b = packets[2 * j, 8:9, :], packets[2 * j + 1, 8:9, :]
            norm_mas[j : j + 1, :] = jnp.where(low, a, turn(b))
            norm_mem[j : j + 1, :] = jnp.where(low, turn(a), b)
        state = hold_rate * norm_mem[...] + mean
        stepped = norm_mas[...] - learn_rate * state
        cn_v[...] = stepped.astype(BF16)
        row = lax.broadcasted_iota(jnp.int32, (8, 128), 0) == z
        pick = lambda v: jnp.sum(jnp.where(row, v, 0.0), axis=0, keepdims=True)
        a, b = pick(stepped), pick(state)
        core0 = lax.broadcast_in_dim(c, (1, 128), ()) == 0
        own_v[...] = jnp.where(low, jnp.where(core0, a, turn(a)), jnp.where(core0, turn(b), b))
        go(pltpu.make_async_copy(cn_v, cn, norm_sem.at[0]))
        go(pltpu.make_async_copy(own_v, own_n, norm_sem.at[1]))

    acts = {"rs": rs_send, "ag": ag_step, "sum": sum_up, "master": master, "update": update, "norm_out": norm_out, "norm_in": norm_in}
    for name, *args in plan()[0]:
        acts[name](*args)

    for copy in delivered + gifts:
        copy.wait_recv()
        copy.wait_send()
    for copy in pending_sends:
        copy.wait_send()
    for copy in pending:
        copy.wait()


def call(pg, pu, pd, pk, mg, mu, md, eg, eu, ed):
    S = jax.ShapeDtypeStruct
    dma = pltpu.SemaphoreType.DMA
    outs = (
        S((Z, 2, ROWS, COLS), BF16), S((Z, 2, ROWS, COLS), BF16), S((2 * HALF, 128 * Z), BF16), S((8, 128), BF16),
        S((ROWS, COLS), F32), S((ROWS, COLS), F32), S((2 * HALF, 64), F32),
        S((ROWS, COLS), F32), S((ROWS, COLS), F32), S((2 * HALF, 64), F32), S((1, 128), F32),
    )
    v = pltpu.VMEM
    scratch = [
        v((2, Z, ROWS, COLS), F32), v((2, Z, ROWS, COLS), F32), v((Z, HALF, 128), F32), v((Z, HALF, 128), F32),
        v((2, 2, 2, 4, 32, COLS), BF16), v((2, 2, 2, 4, 32, COLS), BF16), v((2, 2, 4, 192, 128), BF16), v((2, 2, 4, 192, 128), BF16),
        v((2, Z, ROWS, COLS), BF16), v((Z, HALF, 128), BF16),
        v((2, ROWS, COLS), F32), v((HALF, 128), F32),
        v((2, ROWS, COLS), F32), v((2, ROWS, COLS), F32), v((2 * HALF, 64), F32), v((2 * HALF, 64), F32), v((HALF, 64), F32), v((HALF, 64), F32),
        v((2, 2, ROWS, COLS), F32), v((2, HALF, 64), F32), v((2, HALF, 64), F32),
        v((2, 2, X, ROWS, 128), F32), v((2, 2 * X, 8, 128), F32),
        v((16, 128), F32), v((2 * Z, 16, 128), F32), v((8, 128), F32), v((8, 128), F32), v((8, 128), BF16), v((1, 128), F32),
        dma((3, Z)), dma((3, Z)), dma((3, Z)), dma((3, 2, 2, 4)), dma((3, 2, 2, 4)), dma((3, 2, 2, 4)), dma((3, 2, 2, 4)),
        dma((3, Z, 2)), dma((3, Z, 2)), dma((3, Z, 2)), dma((3, 2)), dma((2,)), dma((2,)),
        dma((2, 3, 2 * X)), dma((2, 3, 2 * X)), dma(()), dma((2 * Z,)), dma((2 * Z,)), dma((3, 2)), dma((2,)), dma((2,)), dma((2,)),
    ]
    any_ = pl.BlockSpec(memory_space=pl.ANY)
    return pl.pallas_call(
        kernel,
        out_shape=outs,
        in_specs=[any_] * 10,
        out_specs=[any_] * len(outs),
        scratch_shapes=scratch,
        compiler_params=pltpu.CompilerParams(collective_id=0, has_side_effects=True, vmem_limit_bytes=48 * 2**20),
    )(pg, pu, pd, pk, mg, mu, md, eg, eu, ed)


def on_device(pg, pu, pd, pn, mg, mu, md, mn, eg, eu, ed, en):
    pk = jnp.concatenate([pn[0], mn, en, jnp.zeros((896,), F32)]).reshape(16, 128)
    cg, cu, cd, cn, sg, su, sd, tg, tu, td, own = call(
        pg.reshape(Z, 2, ROWS, COLS), pu.reshape(Z, 2, ROWS, COLS), pd[0], pk, mg, mu, md, eg, eu, ed
    )
    flat = (2 * Z * ROWS, COLS)
    return (cg.reshape(flat), cu.reshape(flat), cd, cn.reshape(-1), sg, su, sd, own[0, :64], tg, tu, td, own[0, 64:])


def solution(mesh):
    rows, cols = P(("shift", "replica"), "model"), P(("shift", "model"), "replica")
    vec = P(("shift", "replica"))
    return jax.shard_map(
        on_device,
        mesh=mesh,
        in_specs=(
            P(("shift", "replica"), None, "model"), P(("shift", "replica"), None, "model"), P(("shift", "replica"), "model", None),
            P(("shift", "replica"), None), rows, rows, cols, vec, rows, rows, cols, vec,
        ),
        out_specs=(
            P("shift", "model"), P("shift", "model"), P(("shift", "model"), None), P("shift"),
            rows, rows, cols, vec, rows, rows, cols, vec,
        ),
        check_vma=False,
    )
```

time: 189 us -> 89 us (0.47)
  waiting for transfers between devices: 110 us -> 0 us
  Pallas kernels: 0 us -> 69.4 us
  local copies, waits for them, and re-layouts: 37.7 us -> 18.6 us
  starting transfers between devices: 14 us -> 0 us
  between operations: 14.2 us -> 0.69 us
  other arithmetic: 12.1 us -> 0 us
    pallas_call x0 -> x1, Pallas kernels: none -> 69.4 us  [call(): pl.pallas_call(kernel, out_shape=outs, in_specs=[any_] * 10, out_specs=[a...]
    reduce_scatter x1 -> x0, waiting for transfers between devices: 54.7 us -> none  [sum_together(): lax.psum_scatter(lines, axis, tiled=True).reshape(-1)]
    all_gather x1 -> x0, waiting for transfers between devices: 44.7 us -> none  [rows_first(): filled, at, outs = (lax.all_gather(both, axis, axis=0, tiled=True), 0, [])]
    reshape x7 -> x0, local copies, waits for them, and re-layouts: 15.8 us -> none  [the longest x1 10.4 us: sum_together(): jnp.pad(lines, ((0, 0), (0, width * 128 - lines.shape[1]))).reshape(-1, 128)]
    all_to_all x2 -> x0, starting transfers between devices: 14 us -> none  [from_everyone(): return lax.all_to_all(copies, axis, split_axis=0, concat_axis=0, tiled=True)]
    unnamed x20 -> x32, local copies, waits for them, and re-layouts: 4.64 us -> 17.3 us
    all_to_all x2 -> x0, waiting for transfers between devices: 10.8 us -> none  [from_everyone(): return lax.all_to_all(copies, axis, split_axis=0, concat_axis=0, tiled=True)]
    transpose x2 -> x0, local copies, waits for them, and re-layouts: 8.44 us -> none  [the longest x1 4.33 us: rows_first(): outs.append(jnp.moveaxis(section, 0, dim))]
  transfers between devices with their start and end apart: 4 -> 0, of which waited for: 4 -> 0; matrix products, arithmetic and copies ran while one was open for 1% -> 0% of each run, Pallas kernels for 0% -> 0%
where the time goes in v1:
time: 89 us; the launch traced here: 88.7 us
  Pallas kernels  69.4 us (78%)
  local copies, waits for them, and re-layouts  18.6 us (21%)
    pallas_call x1, Pallas kernels, call(): pl.pallas_call(kernel, out_shape=outs, in_specs=[any_] * 10, out_specs=[a...  69.4 us
    unnamed x32, local copies, waits for them, and re-layouts  17.3 us

profile of v1, /device:TPU:1, one launch (start us, length us, event | category | flops | bytes accessed | tf_op | source)
XLA Modules:
  0.0 88.7 jit_solution(11962884276166854803)
XLA Ops:
  0.7 0.8 concatenate.3
  1.4 1.1 %copy.24.refs_6_ = f32[768,64]{1,0:T(8,128)S(1)} copy(f32[768,64]{0,1:T(8,128)} %param.18) | data formatting | bytes 393216 | tf_op args[6]
  2.5 1.1 %copy.25.refs_9_ = f32[768,64]{1,0:T(8,128)S(1)} copy(f32[768,64]{0,1:T(8,128)} %param.22) | data formatting | bytes 393216 | tf_op args[10]
  3.6 0.0 copy-start.4
  3.6 0.9 %copy-done.4 = f32[64,768]{1,0:T(8,128)S(1)} copy-done((f32[64,768]{1,0:T(8,128)S(1)}, f32[64,768]{1,0:T(8,128)}, u32[]{:S(2)}) %copy-start.4) | copy-done | bytes 196632
  4.5 0.0 copy-start.5
  4.5 0.9 %copy-done.5 = f32[64,768]{1,0:T(8,128)S(1)} copy-done((f32[64,768]{1,0:T(8,128)S(1)}, f32[64,768]{1,0:T(8,128)}, u32[]{:S(2)}) %copy-start.5) | copy-done | bytes 196632
  5.5 0.0 copy-start.6
  5.5 0.9 %copy-done.6 = f32[64,768]{1,0:T(8,128)S(1)} copy-done((f32[64,768]{1,0:T(8,128)S(1)}, f32[64,768]{1,0:T(8,128)}, u32[]{:S(2)}) %copy-start.6) | copy-done | bytes 196632
  6.4 0.0 copy-start.7
  6.4 0.9 %copy-done.7 = f32[64,768]{1,0:T(8,128)S(1)} copy-done((f32[64,768]{1,0:T(8,128)S(1)}, f32[64,768]{1,0:T(8,128)}, u32[]{:S(2)}) %copy-start.7) | copy-done | bytes 196632
  7.3 69.4 %shard_map.211 = (bf16[8,2,64,768]{3,2,1,0:T(8,128)(2,1)S(1)}, bf16[8,2,64,768]{3,2,1,0:T(8,128)(2,1)}, bf16[768,1024]{1,0:T(8,128)(2,1)}, bf16[8,128]{1,0:T(8,1...) custom-call(f32[8,2,64,768]{3,2,1,0:T(8,128)} %bitcast.15, ...), custom_call_target="tpu_custom_call" | custom-call | tf_op jit(solution)/shard_map/pallas_call | solution.py:468
  76.7 0.0 copy-start
  76.7 0.7 copy-done
  77.4 0.0 copy-start.2
  77.4 0.7 copy-done.2
  78.1 0.6 slice_bitcast_fusion
  78.7 0.8 copy.26
  79.5 0.8 copy.27
  80.3 0.0 copy-start.9
  80.3 1.1 %copy.36 = bf16[1024,768]{1,0:T(8,128)(2,1)} copy(bf16[1024,768]{1,0:T(8,128)(2,1)S(1)} %bitcast.12) | data formatting | bytes 3145728
  81.5 0.8 copy-done.9
  82.3 0.0 copy-start.8
  82.3 1.1 %copy.37 = bf16[1024,768]{1,0:T(8,128)(2,1)} copy(bf16[1024,768]{1,0:T(8,128)(2,1)S(1)} %bitcast.18) | data formatting | bytes 3145728
  83.4 0.8 copy-done.8
  84.3 0.0 copy-start.3
  84.3 0.0 copy-start.1
  84.3 1.1 %copy.38 = bf16[768,1024]{1,0:T(8,128)(2,1)} copy(bf16[768,1024]{1,0:T(8,128)(2,1)S(1)} %copy-done.8) | data formatting | bytes 3145728
  85.4 0.6 copy.39
  86.0 0.0 copy-done.3
  86.0 0.7 copy.40
  86.7 0.0 copy-done.1
  86.7 0.7 copy.41
  87.3 0.7 copy.42
  88.0 0.7 copy.43
  (1 shorter events, 0.0 us)
Async XLA Ops:
  3.6 0.9 %copy-start.4 = (f32[64,768]{1,0:T(8,128)S(1)}, f32[64,768]{1,0:T(8,128)}, u32[]{:S(2)}) copy-start(f32[64,768]{1,0:T(8,128)} %refs_4_.1) | copy-start | bytes 589828
  4.5 0.9 %copy-start.5 = (f32[64,768]{1,0:T(8,128)S(1)}, f32[64,768]{1,0:T(8,128)}, u32[]{:S(2)}) copy-start(f32[64,768]{1,0:T(8,128)} %refs_5_.1) | copy-start | bytes 589828
  5.5 0.9 %copy-start.6 = (f32[64,768]{1,0:T(8,128)S(1)}, f32[64,768]{1,0:T(8,128)}, u32[]{:S(2)}) copy-start(f32[64,768]{1,0:T(8,128)} %refs_7_.1) | copy-start | bytes 589828
  6.4 0.9 %copy-start.7 = (f32[64,768]{1,0:T(8,128)S(1)}, f32[64,768]{1,0:T(8,128)}, u32[]{:S(2)}) copy-start(f32[64,768]{1,0:T(8,128)} %refs_8_.1) | copy-start | bytes 589828
  76.7 0.7 copy-start
  77.4 0.7 copy-start.2
  80.3 2.0 %copy-start.9 = (bf16[8,2,64,768]{3,2,1,0:T(8,128)(2,1)S(1)}, bf16[8,2,64,768]{3,2,1,0:T(8,128)(2,1)}, u32[]{:S(2)}) copy-start(bf16[8,2,64,768]{3,2,1,0:T(8,128)(2,1)} %get-tuple-element.24) | copy-start | bytes 4718596
  82.3 2.0 %copy-start.8 = (bf16[768,1024]{1,0:T(8,128)(2,1)S(1)}, bf16[768,1024]{1,0:T(8,128)(2,1)}, u32[]{:S(2)}) copy-start(bf16[768,1024]{1,0:T(8,128)(2,1)} %get-tuple-element.62) | copy-start | bytes 4718596
  84.3 1.7 %copy-start.3 = (f32[64,768]{1,0:T(8,128)S(1)}, f32[64,768]{1,0:T(8,128)}, u32[]{:S(2)}) copy-start(f32[64,768]{1,0:T(8,128)} %copy-done.2) | copy-start | bytes 589828
  84.3 2.4 %copy-start.1 = (f32[64,768]{1,0:T(8,128)S(1)}, f32[64,768]{1,0:T(8,128)}, u32[]{:S(2)}) copy-start(f32[64,768]{1,0:T(8,128)} %copy-done) | copy-start | bytes 589828

commit v2 on v1

--- a/solution.py
+++ b/solution.py
@@ -50,11 +50,8 @@
                     needs = [("got", "rs", t, d, h, k + 1)] if k < top else []
                     needs.append(("in", t, STEP[d] * k % Z))
                     tasks["rs", t, d, h, k] = (needs, 0.3 if k < top else 0.2, d, 100 + 10 * k - 3 * t)
-                for k in range(1, top + 1):
-                    needs = [("did", "update", t)] if k == 1 else []
-                    if k > 1:
-                        needs = [("got", "ag", t, d, h, k - 1)]
-                    tasks["ag", t, d, h, k] = (needs, 0.05, d, 50 - 5 * k - t)
+                for k in range(2, top + 1):
+                    tasks["ag", t, d, h, k] = ([("got", "ag", t, d, h, k - 1)], 0.05, d, 50 - 5 * k - t)
                 tasks["ag", t, d, h, top + 1] = ([("got", "ag", t, d, h, top)], 0.05, None, 10)
         ends = [("got", "rs", t, d, h, 1) for d in range(2) for h in range(2)]
         tasks["sum", t] = (ends + [("in", t, 0)], 0.5, None, 200)
@@ -91,27 +88,29 @@
         now += cost
         done[pick] = now
         order.append(pick)
-        if link is not None:
+        sent = [(pick, link)] if link is not None else []
+        if pick[0] == "update":
+            sent = [(("ag", pick[1], d, h, 1), d) for h in range(2) for d in range(2)]
+        for name, link in sent:
             free[link] = max(free[link], now) + wire
-            arrive[pick] = free[link] + lag
+            arrive[name] = free[link] + lag
     return order, now
 
 
 def kernel(*refs):
     it = iter(refs)
     take = lambda n: [next(it) for _ in range(n)]
-    pg, pu, pd, pk, mg, mu, md, eg, eu, ed = take(10)
-    cg, cu, cd, cn, sg, su, sd, tg, tu, td, own_n = take(11)
+    pg, pu, pd, pn, mg, mu, md, mn, eg, eu, ed, en = take(12)
+    cg, cu, cd, cn, sg, su, sd, sn, tg, tu, td, tn = take(12)
     own_gu, peer_gu, own_d, peer_d = take(4)
     rs_out_gu, rs_in_gu, rs_out_d, rs_in_d = take(4)
-    ag_gu, ag_d = take(2)
     mean_gu, mean_d = take(2)
-    mas_gu, mem_gu, mas_d, mem_d, mas_half, mem_half = take(6)
-    new_gu, new_d, give_d = take(3)
+    mas_gu, mem_gu, mas_d, mem_d = take(4)
+    give_d = take(1)[0]
     sq_gu, sq_d = take(2)
-    packet, packets, norm_mas, norm_mem, cn_v, own_v = take(6)
-    (load_sem, swap_s, swap_r, rs_s, rs_r, ag_s, ag_r, agp_s, agp_r, out_sem, mast_sem, half_s, half_r,
-     sq_s, sq_r, pk_sem, pk_s, pk_r, new_sem, give_s, give_r, norm_sem) = take(22)
+    packet, packets, norm_mas, norm_mem, mn_v, en_v = take(6)
+    (load_sem, swap_s, swap_r, rs_s, rs_r, ag_s, ag_r, agp_s, agp_r, mast_sem, half_s, half_r,
+     sq_s, sq_r, pk_sem, pk_s, pk_r, give_s, give_r) = take(19)
 
     r = lax.axis_index("replica")
     z, c = r // 2, r % 2
@@ -123,13 +122,6 @@
 
     def remote(src, dst, s, rv, dev):
         return pltpu.make_async_remote_copy(src_ref=src, dst_ref=dst, send_sem=s, recv_sem=rv, device_id=dev, device_id_type=MESH)
-
-    pending = []
-
-    def go(copy):
-        copy.start()
-        pending.append(copy)
-        return copy
 
     parts = (pg, pu, pd)
 
@@ -164,17 +156,24 @@
             swaps[t, off].start()
 
     masters = {}
-    for t, (m, e) in enumerate(((mg, eg), (mu, eu), (md, ed))):
-        for i, (ref, gu, dn) in enumerate(((m, mas_gu, mas_d), (e, mem_gu, mem_d))):
-            masters[t, i] = pltpu.make_async_copy(ref, gu.at[t] if t < 2 else dn, mast_sem.at[t, i])
+    halves = []
+    half = lambda core: pl.ds(pl.multiple_of(HALF * core, HALF), HALF)
+    mine, theirs = pl.ds(pl.multiple_of(64 * c, 64), 64), pl.ds(pl.multiple_of(64 * (1 - c), 64), 64)
+    for t, pair in enumerate(((mg, eg), (mu, eu), (md, ed))):
+        for i, ref in enumerate(pair):
+            if t < 2:
+                src, dst = ref, (mas_gu, mem_gu)[i].at[t]
+            else:
+                src, dst = ref.at[:, half(c)], (mas_d, mem_d)[i].at[mine]
+                halves.append(remote(ref.at[:, half(1 - c)], dst, half_s.at[i], half_r.at[i], {"replica": peer}))
+                halves[-1].start()
+            masters[t, i] = pltpu.make_async_copy(src, dst, mast_sem.at[t, i])
             masters[t, i].start()
-    halves = []
-    for i, (ref, buf) in enumerate(((md, mas_half), (ed, mem_half))):
-        rows = pl.ds(pl.multiple_of(HALF * (1 - c), HALF), HALF)
-        halves.append(remote(ref.at[rows], buf, half_s.at[i], half_r.at[i], {"replica": peer}))
-        halves[-1].start()
-    load_packet = pltpu.make_async_copy(pk, packet, pk_sem)
-    load_packet.start()
+    load_packet = [
+        pltpu.make_async_copy(ref, dst, pk_sem.at[j]) for j, (ref, dst) in enumerate(((pn, packet.at[:8]), (mn, mn_v), (en, en_v)))
+    ]
+    for copy in load_packet:
+        copy.start()
 
     have = set()
 
@@ -281,103 +280,98 @@
             sq_d[0, 2 * x + c] = total
         share(0, t)
 
-    lane = lax.broadcasted_iota(jnp.int32, (96, 128), 1)
-    mine = lax.broadcast_in_dim(c, (96, 128), ()) == jnp.where(lane < 64, 0, 1)
-
-    def join(own, other):
-        a = jnp.concatenate([own, own], axis=1)
-        b = jnp.concatenate([other, other], axis=1)
-        return jnp.where(mine, a, b)
-
     def master(t):
         masters[t, 0].wait()
         masters[t, 1].wait()
-        n = size(t)
-        if t == 2:
+        if t < 2:
+
+            def body(i, _):
+                here = pl.ds(pl.multiple_of(16 * i, 16), 16)
+                v = mas_gu[t, here, :]
+                sq_gu[1, t, x, here, :] = lanes(v * v)
+                return 0
+
+            lax.fori_loop(0, 4, body, 0)
+        else:
             halves[0].wait_recv()
             halves[1].wait_recv()
             pending_sends.extend(halves)
 
-        def body(i, carry):
-            here = pl.ds(pl.multiple_of(i * n, n), n)
-            if t < 2:
-                v = mas_gu[t, here, :]
-                sq_gu[1, t, x, here, :] = lanes(v * v)
-                return carry
-            there = pl.ds(pl.multiple_of(HALF * c + i * n, n), n)
-            v = join(mas_d[there, :], mas_half[here, :])
-            return carry + eights(v * v)
-
-        total = lax.fori_loop(0, 4, body, jnp.zeros((8, 128), F32))
-        if t == 2:
-            sq_d[1, 2 * x + c] = total
+            def body(i, carry):
+                v = mas_d[:, pl.ds(pl.multiple_of(128 * i, 128), 128)]
+                return carry + v * v
+
+            total = lax.fori_loop(0, HALF // 128, body, jnp.zeros((128, 128), F32))
+            sq_d[1, 2 * x + c] = eights(total.T)
         share(1, t)
 
     def update(t):
         shared(0, t)
         shared(1, t)
-        n = size(t)
-        if t == 2:
-            def ratio_of(w):
-                total = sq_d[w, 0]
-                for j in range(1, 2 * X):
-                    total = total + sq_d[w, j]
-                return jnp.sum(total, axis=0, keepdims=True)
-            ratio_d = jnp.sqrt(ratio_of(1)) * lax.rsqrt(ratio_of(0) + 1e-6)
-
-        def body(i, _):
-            here = pl.ds(pl.multiple_of(i * n, n), n)
-            if t < 2:
+        if t < 2:
+
+            def body(i, _):
+                here = pl.ds(pl.multiple_of(16 * i, 16), 16)
+
                 def whole(w):
                     total = sq_gu[w, t, 0, here, :]
                     for j in range(1, X):
                         total = total + sq_gu[w, t, j, here, :]
                     return jnp.sum(total, axis=1, keepdims=True)
+
                 ratio = jnp.sqrt(whole(1)) * lax.rsqrt(whole(0) + 1e-6)
                 state = hold_rate * mem_gu[t, here, :] + mean_gu[t, here, :] * ratio
                 stepped = mas_gu[t, here, :] - learn_rate * state
-                new_gu[t, 0, here, :] = stepped
-                new_gu[t, 1, here, :] = state
-                ag_gu[t, z, here, :] = stepped.astype(BF16)
+                (sg, su)[t][here, :] = stepped
+                (tg, tu)[t][here, :] = state
+                (cg, cu)[t][z, c, here, :] = stepped.astype(BF16)
                 return 0
-            there = pl.ds(pl.multiple_of(HALF * c + i * n, n), n)
-            state = hold_rate * join(mem_d[there, :], mem_half[here, :]) + mean_d[here, :] * ratio_d
-            stepped = join(mas_d[there, :], mas_half[here, :]) - learn_rate * state
-            ag_d[z, here, :] = stepped.astype(BF16)
-            for j, v in enumerate((stepped, state)):
-                turned = jnp.concatenate([v[:, 64:], v[:, :64]], axis=1)
-                new_d[j, here, :] = jnp.where(mine[:, :64], v[:, :64], turned[:, :64])
-                give_d[j, here, :] = jnp.where(mine[:, :64], turned[:, :64], v[:, :64])
-            return 0
-
-        lax.fori_loop(0, 4, body, 0)
-        if t < 2:
-            for j, ref in enumerate(((sg, su)[t], (tg, tu)[t])):
-                go(pltpu.make_async_copy(new_gu.at[t, j], ref, new_sem.at[t, j]))
+
+            lax.fori_loop(0, 4, body, 0)
         else:
-            rows = pl.ds(pl.multiple_of(HALF * c, HALF), HALF)
+
+            def whole(w):
+                total = sq_d[w, 0]
+                for j in range(1, 2 * X):
+                    total = total + sq_d[w, j]
+                return jnp.sum(total, axis=0, keepdims=True)
+
+            ratio = jnp.sqrt(whole(1)) * lax.rsqrt(whole(0) + 1e-6)
+
+            def body(i, _):
+                here = pl.ds(pl.multiple_of(128 * i, 128), 128)
+                state = hold_rate * mem_d[:, here] + (mean_d[here, :] * ratio).T
+                stepped = mas_d[:, here] - learn_rate * state
+                cd[z, c, here, :] = stepped.T.astype(BF16)
+                there = pl.ds(pl.multiple_of(HALF * c + 128 * i, 128), 128)
+                for j, v in enumerate((stepped, state)):
+                    (sd, td)[j][:, there] = jnp.where(low_core, v[:64], v[64:])
+                    give_d[j, :, here] = jnp.where(low_core, v[64:], v[:64])
+                return 0
+
+            low_core = lax.broadcast_in_dim(c, (64, 128), ()) == 0
+            lax.fori_loop(0, HALF // 128, body, 0)
+        for h in range(2):
+            for d in range(2):
+                ag_step(t, d, h, 1)
+        for h in range(2):
+            deliver(t, 0, h)
+        if t == 2:
             for j, ref in enumerate((sd, td)):
-                go(pltpu.make_async_copy(new_d.at[j], ref.at[rows], new_sem.at[t, j]))
-                gift = remote(give_d.at[j], ref.at[rows], give_s.at[j], give_r.at[j], {"replica": peer})
+                gift = remote(give_d.at[j], ref.at[:, half(c)], give_s.at[j], give_r.at[j], {"replica": peer})
                 gift.start()
                 gifts.append(gift)
-        for h in range(2):
-            deliver(t, 0, h)
 
     gifts = []
-    ag_at = lambda t, at, h: ag_gu.at[t, at, pl.ds(32 * h, 32)] if t < 2 else ag_d.at[at, pl.ds(192 * h, 192)]
-
-    def place(t, at, h, core):
-        if t < 2:
-            return (cg, cu)[t].at[at, core, pl.ds(32 * h, 32)]
-        return cd.at[pl.ds(pl.multiple_of(HALF * core + 192 * h, 192), 192), pl.ds(pl.multiple_of(128 * at, 128), 128)]
+
+    def ag_at(t, at, h):
+        return (cg, cu, cd)[t].at[at, c, pl.ds((32, 32, 192)[t] * h, (32, 32, 192)[t])]
 
     delivered = []
 
     def deliver(t, off, h):
         at = chip(off)
-        go(pltpu.make_async_copy(ag_at(t, at, h), place(t, at, h, c), out_sem.at[t, off % Z, h]))
-        copy = remote(ag_at(t, at, h), place(t, at, h, c), agp_s.at[t, off % Z, h], agp_r.at[t, off % Z, h], {"replica": peer})
+        copy = remote(ag_at(t, at, h), ag_at(t, at, h), agp_s.at[t, off % Z, h], agp_r.at[t, off % Z, h], {"replica": peer})
         copy.start()
         delivered.append(copy)
 
@@ -398,8 +392,12 @@
     def norm_copies():
         return [remote(packet, packets.at[r], pk_s.at[j], pk_r.at[j], {"replica": lax.rem(r + j, 2 * Z)}) for j in range(1, 2 * Z)]
 
+    turn = lambda v: jnp.concatenate([v[:, 64:], v[:, :64]], axis=1)
+
     def norm_out():
-        load_packet.wait()
+        for copy in load_packet:
+            copy.wait()
+        packet[8:9, :] = jnp.concatenate([mn_v[...], en_v[...]], axis=1)
         for copy in norm_copies():
             copy.start()
             pending_sends.append(copy)
@@ -413,21 +411,19 @@
             total = total + packets[j, :8, :]
         mean = total * (2 * Z) ** -0.5
         low = lax.broadcasted_iota(jnp.int32, (1, 128), 1) < 64
-        turn = lambda v: jnp.concatenate([v[:, 64:], v[:, :64]], axis=1)
         for j in range(Z):
             a, b = packets[2 * j, 8:9, :], packets[2 * j + 1, 8:9, :]
             norm_mas[j : j + 1, :] = jnp.where(low, a, turn(b))
             norm_mem[j : j + 1, :] = jnp.where(low, turn(a), b)
         state = hold_rate * norm_mem[...] + mean
         stepped = norm_mas[...] - learn_rate * state
-        cn_v[...] = stepped.astype(BF16)
+        cn[...] = stepped.astype(BF16)
         row = lax.broadcasted_iota(jnp.int32, (8, 128), 0) == z
         pick = lambda v: jnp.sum(jnp.where(row, v, 0.0), axis=0, keepdims=True)
         a, b = pick(stepped), pick(state)
-        core0 = lax.broadcast_in_dim(c, (1, 128), ()) == 0
-        own_v[...] = jnp.where(low, jnp.where(core0, a, turn(a)), jnp.where(core0, turn(b), b))
-        go(pltpu.make_async_copy(cn_v, cn, norm_sem.at[0]))
-        go(pltpu.make_async_copy(own_v, own_n, norm_sem.at[1]))
+        first = lax.broadcast_in_dim(c, (1, 64), ()) == 0
+        sn[...] = jnp.where(first, a[:, :64], turn(a)[:, :64])
+        tn[...] = jnp.where(first, b[:, :64], turn(b)[:, :64])
 
     acts = {"rs": rs_send, "ag": ag_step, "sum": sum_up, "master": master, "update": update, "norm_out": norm_out, "norm_in": norm_in}
     for name, *args in plan()[0]:
@@ -435,53 +431,77 @@
 
     for copy in delivered + gifts:
         copy.wait_recv()
+    for copy in pending_sends + delivered + gifts:
         copy.wait_send()
-    for copy in pending_sends:
-        copy.wait_send()
-    for copy in pending:
+
+
+def write(*refs):
+    src, dst, sem = refs[:12], refs[12:24], refs[24]
+    copies = []
+
+    def put(a, b):
+        copies.append(pltpu.make_async_copy(a, b, sem.at[len(copies)]))
+        copies[-1].start()
+
+    for i in range(12):
+        if i != 2:
+            put(src[i], dst[i])
+            continue
+        for at in range(Z):
+            for core in range(2):
+                put(src[i].at[at, core], dst[i].at[pl.ds(HALF * core, HALF), pl.ds(128 * at, 128)])
+    for copy in copies:
         copy.wait()
 
 
-def call(pg, pu, pd, pk, mg, mu, md, eg, eu, ed):
+def call(*args):
     S = jax.ShapeDtypeStruct
     dma = pltpu.SemaphoreType.DMA
     outs = (
-        S((Z, 2, ROWS, COLS), BF16), S((Z, 2, ROWS, COLS), BF16), S((2 * HALF, 128 * Z), BF16), S((8, 128), BF16),
-        S((ROWS, COLS), F32), S((ROWS, COLS), F32), S((2 * HALF, 64), F32),
-        S((ROWS, COLS), F32), S((ROWS, COLS), F32), S((2 * HALF, 64), F32), S((1, 128), F32),
+        S((Z, 2, ROWS, COLS), BF16), S((Z, 2, ROWS, COLS), BF16), S((Z, 2, HALF, 128), BF16), S((8, 128), BF16),
+        S((ROWS, COLS), F32), S((ROWS, COLS), F32), S((64, 2 * HALF), F32), S((1, 64), F32),
+        S((ROWS, COLS), F32), S((ROWS, COLS), F32), S((64, 2 * HALF), F32), S((1, 64), F32),
     )
     v = pltpu.VMEM
     scratch = [
         v((2, Z, ROWS, COLS), F32), v((2, Z, ROWS, COLS), F32), v((Z, HALF, 128), F32), v((Z, HALF, 128), F32),
         v((2, 2, 2, 4, 32, COLS), BF16), v((2, 2, 2, 4, 32, COLS), BF16), v((2, 2, 4, 192, 128), BF16), v((2, 2, 4, 192, 128), BF16),
-        v((2, Z, ROWS, COLS), BF16), v((Z, HALF, 128), BF16),
         v((2, ROWS, COLS), F32), v((HALF, 128), F32),
-        v((2, ROWS, COLS), F32), v((2, ROWS, COLS), F32), v((2 * HALF, 64), F32), v((2 * HALF, 64), F32), v((HALF, 64), F32), v((HALF, 64), F32),
-        v((2, 2, ROWS, COLS), F32), v((2, HALF, 64), F32), v((2, HALF, 64), F32),
+        v((2, ROWS, COLS), F32), v((2, ROWS, COLS), F32), v((128, HALF), F32), v((128, HALF), F32),
+        v((2, 64, HALF), F32),
         v((2, 2, X, ROWS, 128), F32), v((2, 2 * X, 8, 128), F32),
-        v((16, 128), F32), v((2 * Z, 16, 128), F32), v((8, 128), F32), v((8, 128), F32), v((8, 128), BF16), v((1, 128), F32),
+        v((16, 128), F32), v((2 * Z, 16, 128), F32), v((8, 128), F32), v((8, 128), F32), v((1, 64), F32), v((1, 64), F32),
         dma((3, Z)), dma((3, Z)), dma((3, Z)), dma((3, 2, 2, 4)), dma((3, 2, 2, 4)), dma((3, 2, 2, 4)), dma((3, 2, 2, 4)),
-        dma((3, Z, 2)), dma((3, Z, 2)), dma((3, Z, 2)), dma((3, 2)), dma((2,)), dma((2,)),
-        dma((2, 3, 2 * X)), dma((2, 3, 2 * X)), dma(()), dma((2 * Z,)), dma((2 * Z,)), dma((3, 2)), dma((2,)), dma((2,)), dma((2,)),
+        dma((3, Z, 2)), dma((3, Z, 2)), dma((3, 2)), dma((2,)), dma((2,)),
+        dma((2, 3, 2 * X)), dma((2, 3, 2 * X)), dma((3,)), dma((2 * Z,)), dma((2 * Z,)), dma((2,)), dma((2,)),
     ]
-    any_ = pl.BlockSpec(memory_space=pl.ANY)
-    return pl.pallas_call(
+    any_, hbm = pl.BlockSpec(memory_space=pl.ANY), pl.BlockSpec(memory_space=pltpu.HBM)
+    args = [pltpu.with_memory_space_constraint(a, pltpu.HBM) for a in args]
+    results = pl.pallas_call(
         kernel,
         out_shape=outs,
-        in_specs=[any_] * 10,
-        out_specs=[any_] * len(outs),
+        in_specs=[hbm] * len(args),
+        out_specs=[pl.BlockSpec(memory_space=pltpu.VMEM)] * len(outs),
         scratch_shapes=scratch,
-        compiler_params=pltpu.CompilerParams(collective_id=0, has_side_effects=True, vmem_limit_bytes=48 * 2**20),
-    )(pg, pu, pd, pk, mg, mu, md, eg, eu, ed)
+        compiler_params=pltpu.CompilerParams(collective_id=0, has_side_effects=True, vmem_limit_bytes=28 * 2**20),
+    )(*args)
+    return pl.pallas_call(
+        write,
+        out_shape=outs[:2] + (S((2 * HALF, 128 * Z), BF16),) + outs[3:],
+        in_specs=[any_] * len(outs),
+        out_specs=[hbm] * len(outs),
+        scratch_shapes=[dma((2 * Z + 11,))],
+        compiler_params=pltpu.CompilerParams(vmem_limit_bytes=2**20),
+    )(*results)
 
 
 def on_device(pg, pu, pd, pn, mg, mu, md, mn, eg, eu, ed, en):
-    pk = jnp.concatenate([pn[0], mn, en, jnp.zeros((896,), F32)]).reshape(16, 128)
-    cg, cu, cd, cn, sg, su, sd, tg, tu, td, own = call(
-        pg.reshape(Z, 2, ROWS, COLS), pu.reshape(Z, 2, ROWS, COLS), pd[0], pk, mg, mu, md, eg, eu, ed
+    wide = lambda p: p.reshape(Z, 2, ROWS, COLS)
+    cg, cu, cd, cn, sg, su, sd, sn, tg, tu, td, tn = call(
+        wide(pg), wide(pu), pd[0], pn.reshape(8, 128), mg, mu, md.T, mn.reshape(1, -1), eg, eu, ed.T, en.reshape(1, -1)
     )
     flat = (2 * Z * ROWS, COLS)
-    return (cg.reshape(flat), cu.reshape(flat), cd, cn.reshape(-1), sg, su, sd, own[0, :64], tg, tu, td, own[0, 64:])
+    return (cg.reshape(flat), cu.reshape(flat), cd, cn.reshape(-1), sg, su, sd.T, sn[0], tg, tu, td.T, tn[0])
 
 
 def solution(mesh):

time: 89 us -> 72 us (0.81)
  local copies, waits for them, and re-layouts: 18.6 us -> 0 us
  Pallas kernels: 69.4 us -> 71.2 us
    unnamed x32 -> x0, local copies, waits for them, and re-layouts: 17.3 us -> none
    pallas_call x1 -> x2, Pallas kernels: 69.4 us -> 71.2 us  [the longest x1 68.5 us: call(): pl.pallas_call(kernel, out_shape=outs, in_specs=[hbm] * len(args), out_sp...]
where the time goes in v2:
time: 72 us; the launch traced here: 71.9 us
  Pallas kernels  71.2 us (99%)
    pallas_call x1, Pallas kernels, call(): pl.pallas_call(kernel, out_shape=outs, in_specs=[hbm] * len(args), out_sp...  68.5 us
    pallas_call x1, Pallas kernels, call(): pl.pallas_call(write, out_shape=outs[:2] + (S((2 * HALF, 128 * Z), BF16),...  2.77 us

profile of v2, /device:TPU:1, one launch (start us, length us, event | category | flops | bytes accessed | tf_op | source)
XLA Modules:
  0.0 71.9 jit_solution(9637329759789053108)
XLA Ops:
  0.6 68.5 %shard_map.211 = (bf16[8,2,64,768]{3,2,1,0:T(8,128)(2,1)S(1)}, bf16[8,2,64,768]{3,2,1,0:T(8,128)(2,1)S(1)}, bf16[8,2,384,128]{3,2,1,0:T(8,128)(2,1)S(1)}, bf16[8...) custom-call(f32[8,2,64,768]{3,2,1,0:T(8,128)} %bitcast.15, ...), custom_call_target="tpu_custom_call" | custom-call | tf_op jit(solution)/shard_map/pallas_call | solution.py:480
  69.1 2.8 %shard_map.212 = (bf16[8,2,64,768]{3,2,1,0:T(8,128)(2,1)}, bf16[8,2,64,768]{3,2,1,0:T(8,128)(2,1)}, bf16[768,1024]{1,0:T(8,128)(2,1)}, bf16[8,128]{1,0:T(8,128)(...) custom-call(bf16[8,2,64,768]{3,2,1,0:T(8,128)(2,1)S(1)} %get-tuple-e, ...), custom_call_target="tpu_custom_call" | custom-call | tf_op jit(solution)/shard_map/pallas_call | solution.py:488

commit v3 on v2

v3 whole, which is shorter than its diff:
```python
import functools

import jax
import jax.numpy as jnp
from jax import lax
from jax.experimental import pallas as pl
from jax.experimental.pallas import tpu as pltpu
from jax.sharding import PartitionSpec as P

MESH = pl.DeviceIdType.MESH
F32, BF16 = jnp.float32, jnp.bfloat16
learn_rate = 0.5
hold_rate = 0.9

Z = 8
X = 4
ROWS = 64
COLS = 768
HALF = 384
STEP = (1, -1)
SCALE = 8192.0


AHEAD = 3


def encode(v):
    v = v * SCALE
    a = v * v
    a = a * a
    a = a * a
    return jnp.where(v < 0, -a, a).astype(BF16)


def decode(y):
    y = y.astype(F32)
    a = jnp.abs(y)
    q = lax.rsqrt(lax.rsqrt(jnp.maximum(a, 1e-37)))
    x = q * lax.rsqrt(q) * (1.0 / SCALE)
    x = jnp.where(a < 2e-37, 0.0, x)
    return jnp.where(y < 0, -x, x)


ORDER = (
    "r0L4", "r0S3", "r2L4", "r1L4", "r0L3", "r0S2", "m0", "r2L3", "r1L3", "m1", "r0L2", "r1S3", "m2", "r0S1", "r1L2",
    "r0L1", "r1S2", "r2S3", "r2L2", "s0", "n0", "r1L1", "r1S1", "r2S2", "r2L1", "u0", "s1", "r2S1", "a0L2", "a0S2", "n1",
    "u1", "s2", "a0L3", "a0S3", "a1L2", "u2", "a1S2", "a1L3", "a2L2", "a0L4", "a2S2", "a2L3", "a1L4", "a1S3",
    "a0L5", "a2S3", "a2L4", "a1L5", "n2", "a2S4", "a1S4", "a0S4", "a2L5",
)
TOP = {"L": 4, "S": 3}


def slot(p, k):
    return TOP[p] - k + (0 if p == "L" else 4)


def kernel(*refs):
    it = iter(refs)
    take = lambda n: [next(it) for _ in range(n)]
    pg, pu, pd, pn, mg, mu, md, mn, eg, eu, ed, en = take(12)
    cg, cu, cd, cn, sg, su, sd, sn, tg, tu, td, tn = take(12)
    own_gu, peer_gu, own_d, peer_d = take(4)
    rs_out_gu, rs_in_gu, rs_out_d, rs_in_d = take(4)
    mean_gu, mean_d = take(2)
    mas_gu, mem_gu, mas_d, mem_d = take(4)
    give_d = take(1)[0]
    sq_gu, sq_d = take(2)
    pn_v, mn_v, en_v, row_out, row_in, row_new = take(6)
    (in_sem, swap_s, rs_s, rs_r, ag_s, ag_r, agp_s, agp_r, mast_sem, half_s, half_r,
     sq_s, sq_r, pk_sem, pk_s, row_s, row_r, give_s, give_r) = take(19)

    r = lax.axis_index("replica")
    z, c = r // 2, r % 2
    peer = r + 1 - 2 * c
    x = lax.axis_index("model")
    chip = lambda off: lax.rem(z + off + 2 * Z, Z)
    beside = lambda d: {"replica": 2 * chip(STEP[d]) + c}
    across = lambda i: lax.rem(x + i, X)

    def remote(src, dst, s, rv, dev):
        return pltpu.make_async_remote_copy(src_ref=src, dst_ref=dst, send_sem=s, recv_sem=rv, device_id=dev, device_id_type=MESH)

    parts = (pg, pu, pd)

    def block(t, at, core):
        if t < 2:
            return parts[t].at[at, core]
        return pd.at[pl.ds(pl.multiple_of(HALF * core, HALF), HALF), pl.ds(pl.multiple_of(128 * at, 128), 128)]

    own_at = lambda t, at: own_gu.at[t, at] if t < 2 else own_d.at[at]
    peer_at = lambda t, at: peer_gu.at[t, at] if t < 2 else peer_d.at[at]
    ends = lambda lev: (lev,) if lev in (0, 4) else (lev, -lev)
    needed = []
    for code in ORDER:
        lev = int(code[3]) if code[0] == "r" else 0
        if code[0] in "rs" and (int(code[1]), lev) not in needed:
            needed.append((int(code[1]), lev))
    for t, lev in needed:
        for off in ends(lev):
            pltpu.make_async_copy(block(t, chip(off), c), own_at(t, chip(off)), in_sem.at[t, lev]).start()

    barrier = pltpu.get_barrier_semaphore()
    hello = [{"replica": peer}, beside(0), beside(1)]
    for i in range(1, X):
        hello.append({"model": across(i)})
        hello.append({"replica": peer, "model": across(i)})
    for dev in hello:
        pl.semaphore_signal(barrier, inc=1, device_id=dev, device_id_type=MESH)
    pl.semaphore_wait(barrier, len(hello))

    def await_in(ref, sem):
        remote(ref, ref, sem, sem, {"replica": peer}).wait_recv()

    def await_out(ref, sem):
        remote(ref, ref, sem, sem, {"replica": peer}).wait_send()

    swapped = []

    def swap(ahead):
        while len(swapped) < min(ahead, len(needed)):
            t, lev = needed[len(swapped)]
            for off in ends(lev):
                at = chip(off)
                remote(block(t, at, 1 - c), peer_at(t, at), swap_s.at[t // 2], in_sem.at[t, lev], {"replica": peer}).start()
            swapped.append((t, lev))

    have = []

    def need(t, lev):
        if (t, lev) not in have:
            have.append((t, lev))
            n = 2 * len(ends(lev))
            await_in(own_gu.at[0, pl.ds(0, n)] if t < 2 else own_d.at[pl.ds(0, n)], in_sem.at[t, lev])
            swap(len(have) + AHEAD)

    swap(AHEAD)

    half = lambda core: pl.ds(pl.multiple_of(HALF * core, HALF), HALF)
    mine, theirs = pl.ds(pl.multiple_of(64 * c, 64), 64), pl.ds(pl.multiple_of(64 * (1 - c), 64), 64)
    for t, pair in enumerate(((mg, eg), (mu, eu), (md, ed))):
        for i, ref in enumerate(pair):
            if t < 2:
                src, dst = ref, (mas_gu, mem_gu)[i].at[t]
            else:
                src, dst = ref.at[:, half(c)], (mas_d, mem_d)[i].at[mine]
                remote(ref.at[:, half(1 - c)], dst, half_s, half_r, {"replica": peer}).start()
            pltpu.make_async_copy(src, dst, mast_sem.at[t]).start()
    vectors = ((pn, pn_v), (mn, mn_v), (en, en_v))
    for j, (ref, buf) in enumerate(vectors):
        pltpu.make_async_copy(ref, buf.at[0], pk_sem.at[j]).start()
        remote(ref, buf.at[1], pk_s.at[j], pk_sem.at[j], {"replica": peer}).start()

    rs_out = lambda t, j: rs_out_gu.at[t, j] if t < 2 else rs_out_d.at[j]
    rs_in = lambda t, j: rs_in_gu.at[t, j] if t < 2 else rs_in_d.at[j]
    piece = lambda p, d: 1 - d if p == "L" else d

    size = lambda t: 16 if t < 2 else 96

    def rs_send(t, p, k):
        need(t, k)
        n, j = size(t), slot(p, k)
        chained = k < TOP[p]
        if chained:
            await_in(rs_in(t, j - 1), rs_r.at[t, j - 1])
        for d in range(2):
            at, h = chip(STEP[d] * k), piece(p, d)
            own, other, out = own_at(t, at), peer_at(t, at), rs_out(t, j).at[d]
            arrived = rs_in(t, j - 1).at[d] if chained else None

            def body(i, _):
                here = pl.ds(pl.multiple_of(i * n, n), n)
                there = pl.ds(pl.multiple_of(2 * n * h + i * n, n), n)
                v = own[there, :] + other[there, :]
                if chained:
                    v = v + decode(arrived[here, :])
                out[here, :] = encode(v)
                return 0

            lax.fori_loop(0, 2, body, 0)
            remote(out, rs_in(t, j).at[d], rs_s.at[t // 2], rs_r.at[t, j], beside(d)).start()

    def sq_slot(w, t):
        return sq_gu.at[w, t, x] if t < 2 else sq_d.at[w, 2 * x + c]

    def sq_copies(w, t):
        to = [{"model": across(i)} for i in range(1, X)]
        if t == 2:
            to += [{"replica": peer, "model": across(i)} for i in range(X)]
        return [remote(sq_slot(w, t), sq_slot(w, t), sq_s.at[t], sq_r.at[t], dev) for dev in to]

    def share(w, t):
        for copy in sq_copies(w, t):
            copy.start()

    sq_all = lambda t: sq_gu.at[:, t, pl.ds(0, X - 1)] if t < 2 else sq_d.at[:, pl.ds(0, 2 * X - 1)]

    def lanes(v):
        total = v[:, :128]
        for j in range(1, v.shape[1] // 128):
            total = total + v[:, 128 * j : 128 * (j + 1)]
        return total

    def eights(v):
        total = v[:8]
        for j in range(1, v.shape[0] // 8):
            total = total + v[8 * j : 8 * (j + 1)]
        return total

    def sum_up(t):
        need(t, 0)
        for p in "LS":
            await_in(rs_in(t, slot(p, 1)), rs_r.at[t, slot(p, 1)])
        n = size(t)
        own, other = own_at(t, z), peer_at(t, z)
        for h in range(2):
            ahead, back = (rs_in(t, slot("L" if piece("L", d) == h else "S", 1)).at[d] for d in range(2))

            def body(i, carry):
                here = pl.ds(pl.multiple_of(i * n, n), n)
                there = pl.ds(pl.multiple_of(2 * n * h + i * n, n), n)
                v = (own[there, :] + other[there, :]) + (decode(ahead[here, :]) + decode(back[here, :]))
                v = v * (2 * Z) ** -0.5
                if t < 2:
                    mean_gu[t, there, :] = v
                    sq_gu[0, t, x, there, :] = lanes(v * v)
                    return carry
                mean_d[there, :] = v
                return carry + eights(v * v)

            first = jnp.zeros((8, 128), F32) if h == 0 else total
            total = lax.fori_loop(0, 2, body, first)
        if t == 2:
            sq_d[0, 2 * x + c] = total
        share(0, t)

    def master(t):
        await_in(mean_gu if t < 2 else mas_d, mast_sem.at[t])
        if t < 2:

            def body(i, _):
                here = pl.ds(pl.multiple_of(16 * i, 16), 16)
                v = mas_gu[t, here, :]
                sq_gu[1, t, x, here, :] = lanes(v * v)
                return 0

            lax.fori_loop(0, 4, body, 0)
        else:
            await_in(mas_d, half_r)

            def body(i, carry):
                v = mas_d[:, pl.ds(pl.multiple_of(128 * i, 128), 128)]
                return carry + v * v

            total = lax.fori_loop(0, HALF // 128, body, jnp.zeros((128, 128), F32))
            sq_d[1, 2 * x + c] = eights(total.T)
        share(1, t)

    def update(t):
        await_in(sq_all(t), sq_r.at[t])
        if t < 2:

            def body(i, _):
                here = pl.ds(pl.multiple_of(16 * i, 16), 16)

                def whole(w):
                    total = sq_gu[w, t, 0, here, :]
                    for j in range(1, X):
                        total = total + sq_gu[w, t, j, here, :]
                    return jnp.sum(total, axis=1, keepdims=True)

                ratio = jnp.sqrt(whole(1)) * lax.rsqrt(whole(0) + 1e-6)
                state = hold_rate * mem_gu[t, here, :] + mean_gu[t, here, :] * ratio
                stepped = mas_gu[t, here, :] - learn_rate * state
                (sg, su)[t][here, :] = stepped
                (tg, tu)[t][here, :] = state
                (cg, cu)[t][z, c, here, :] = stepped.astype(BF16)
                return 0

            lax.fori_loop(0, 4, body, 0)
        else:

            def whole(w):
                total = sq_d[w, 0]
                for j in range(1, 2 * X):
                    total = total + sq_d[w, j]
                return jnp.sum(total, axis=0, keepdims=True)

            ratio = jnp.sqrt(whole(1)) * lax.rsqrt(whole(0) + 1e-6)

            def body(i, _):
                here = pl.ds(pl.multiple_of(128 * i, 128), 128)
                state = hold_rate * mem_d[:, here] + (mean_d[here, :] * ratio).T
                stepped = mas_d[:, here] - learn_rate * state
                cd[z, c, here, :] = stepped.T.astype(BF16)
                there = pl.ds(pl.multiple_of(HALF * c + 128 * i, 128), 128)
                for j, v in enumerate((stepped, state)):
                    (sd, td)[j][:, there] = jnp.where(low_core, v[:64], v[64:])
                    give_d[j, :, here] = jnp.where(low_core, v[64:], v[:64])
                return 0

            low_core = lax.broadcast_in_dim(c, (64, 128), ()) == 0
            lax.fori_loop(0, HALF // 128, body, 0)
        for p in "LS":
            ag_send(t, p, 1)
        for h in range(2):
            deliver(t, 0, h)
        if t == 2:
            for j, ref in enumerate((sd, td)):
                remote(give_d.at[j], ref.at[:, half(c)], give_s, give_r, {"replica": peer}).start()


    def ag_at(t, at, h):
        return (cg, cu, cd)[t].at[at, c, pl.ds((32, 32, 192)[t] * h, (32, 32, 192)[t])]

    def deliver(t, off, h):
        at = ag_at(t, chip(off), h)
        remote(at, at, agp_s.at[t], agp_r.at[t], {"replica": peer}).start()

    def ag_send(t, p, k):
        for d in range(2):
            at = ag_at(t, chip(-STEP[d] * (k - 1)), piece(p, d))
            remote(at, at, ag_s.at[t], ag_r.at[t, slot(p, k)], beside(d)).start()

    def ag_step(t, p, k):
        await_in((cg, cu, cd)[t].at[0, 0], ag_r.at[t, slot(p, k - 1)])
        if k <= TOP[p]:
            ag_send(t, p, k)
        for d in range(2):
            deliver(t, -STEP[d] * (k - 1), piece(p, d))

    turn = lambda v: jnp.concatenate([v[:, 64:], v[:, :64]], axis=1)
    core0 = lambda n: lax.broadcast_in_dim(c, (1, n), ()) == 0

    def rows_to(src, dst, j):
        for off in range(1, Z):
            remote(src(off), dst.at[z], row_s.at[j], row_r.at[j], {"replica": 2 * chip(off) + c}).start()

    def norm_parts():
        for j, (_, buf) in enumerate(vectors):
            await_in(buf, pk_sem.at[j])
        for j in range(Z):
            row_out[j] = pn_v[0, j : j + 1, :] + pn_v[1, j : j + 1, :]
        row_in[z] = row_out[z]
        rows_to(lambda off: row_out.at[chip(off)], row_in, 0)

    def norm_step():
        await_in(row_out.at[pl.ds(0, Z - 1)], row_r.at[0])
        total = row_in[0]
        for j in range(1, Z):
            total = total + row_in[j]

        def both(ref):
            a, b = jnp.concatenate([ref[0], ref[1]], axis=1), jnp.concatenate([ref[1], ref[0]], axis=1)
            return jnp.where(core0(128), a, b)

        state = hold_rate * both(en_v) + total * (2 * Z) ** -0.5
        stepped = both(mn_v) - learn_rate * state
        row_new[z] = stepped
        rows_to(lambda off: row_new.at[z], row_new, 1)
        sn[...] = jnp.where(core0(64), stepped[:, :64], turn(stepped)[:, :64])
        tn[...] = jnp.where(core0(64), state[:, :64], turn(state)[:, :64])

    def norm_all():
        await_in(row_out.at[pl.ds(0, Z - 1)], row_r.at[1])
        cn[...] = jnp.concatenate([row_new[j] for j in range(Z)], axis=0).astype(BF16)

    for code in ORDER:
        kind, t = code[0], int(code[1])
        with jax.named_scope(code):
            if kind == "r":
                rs_send(t, code[2], int(code[3]))
            elif kind == "a":
                ag_step(t, code[2], int(code[3]))
            elif kind == "n":
                (norm_parts, norm_step, norm_all)[t]()
            else:
                {"s": sum_up, "m": master, "u": update}[kind](t)

    for t in range(3):
        await_in((cg, cu, cd)[t].at[:, 0], agp_r.at[t])
    await_in(give_d, give_r)
    for j in range(2):
        await_out((peer_gu, peer_d)[j], swap_s.at[j])
        await_out((rs_out_gu, rs_out_d)[j], rs_s.at[j])
    for t in range(3):
        await_out((cg, cu, cd)[t].at[pl.ds(0, 7), 0], ag_s.at[t])
        await_out((cg, cu, cd)[t].at[:, 0], agp_s.at[t])
        await_out(sq_all(t), sq_s.at[t])
    await_out(mas_d, half_s)
    for j, (ref, buf) in enumerate(vectors):
        await_out(buf.at[1], pk_s.at[j])
    for j in range(2):
        await_out(row_out.at[pl.ds(0, Z - 1)], row_s.at[j])
    await_out(give_d, give_s)


def write(*refs):
    src, dst, sem = refs[:12], refs[12:24], refs[24]
    copies = []

    for at in range(Z):
        for core in range(2):
            there = dst[2].at[pl.ds(HALF * core, HALF), pl.ds(128 * at, 128)]
            pltpu.make_async_copy(src[2].at[at, core], there, sem.at[2]).start()
    for i in range(12):
        if i != 2:
            copies.append(pltpu.make_async_copy(src[i], dst[i], sem.at[i]))
            copies[-1].start()
    for copy in copies:
        copy.wait()
    pltpu.make_async_copy(dst[2], dst[2], sem.at[2]).wait()


def call(*args):
    S = jax.ShapeDtypeStruct
    dma = pltpu.SemaphoreType.DMA
    outs = (
        S((Z, 2, ROWS, COLS), BF16), S((Z, 2, ROWS, COLS), BF16), S((Z, 2, HALF, 128), BF16), S((8, 128), BF16),
        S((ROWS, COLS), F32), S((ROWS, COLS), F32), S((64, 2 * HALF), F32), S((1, 64), F32),
        S((ROWS, COLS), F32), S((ROWS, COLS), F32), S((64, 2 * HALF), F32), S((1, 64), F32),
    )
    v = pltpu.VMEM
    scratch = [
        v((2, Z, ROWS, COLS), F32), v((2, Z, ROWS, COLS), F32), v((Z, HALF, 128), F32), v((Z, HALF, 128), F32),
        v((2, 7, 2, 32, COLS), BF16), v((2, 7, 2, 32, COLS), BF16), v((7, 2, 192, 128), BF16), v((7, 2, 192, 128), BF16),
        v((2, ROWS, COLS), F32), v((HALF, 128), F32),
        v((2, ROWS, COLS), F32), v((2, ROWS, COLS), F32), v((128, HALF), F32), v((128, HALF), F32),
        v((2, 64, HALF), F32),
        v((2, 2, X, ROWS, 128), F32), v((2, 2 * X, 8, 128), F32),
        v((2, 8, 128), F32), v((2, 1, 64), F32), v((2, 1, 64), F32), v((Z, 1, 128), F32), v((Z, 1, 128), F32), v((Z, 1, 128), F32),
        dma((3, 5)), dma((2,)), dma((2,)), dma((3, 7)), dma((3,)), dma((3, 7)), dma((3,)), dma((3,)), dma((3,)), dma(()), dma(()),
        dma((3,)), dma((3,)), dma((3,)), dma((3,)), dma((2,)), dma((2,)), dma(()), dma(()),
    ]
    any_, hbm = pl.BlockSpec(memory_space=pl.ANY), pl.BlockSpec(memory_space=pltpu.HBM)
    args = [pltpu.with_memory_space_constraint(a, pltpu.HBM) for a in args]
    results = pl.pallas_call(
        kernel,
        out_shape=outs,
        in_specs=[hbm] * len(args),
        out_specs=[pl.BlockSpec(memory_space=pltpu.VMEM)] * len(outs),
        scratch_shapes=scratch,
        compiler_params=pltpu.CompilerParams(collective_id=0, has_side_effects=True, vmem_limit_bytes=28 * 2**20),
    )(*args)
    return pl.pallas_call(
        write,
        out_shape=outs[:2] + (S((2 * HALF, 128 * Z), BF16),) + outs[3:],
        in_specs=[any_] * len(outs),
        out_specs=[hbm] * len(outs),
        scratch_shapes=[dma((12,))],
        compiler_params=pltpu.CompilerParams(vmem_limit_bytes=2**20),
    )(*results)


def on_device(pg, pu, pd, pn, mg, mu, md, mn, eg, eu, ed, en):
    wide = lambda p: p.reshape(Z, 2, ROWS, COLS)
    cg, cu, cd, cn, sg, su, sd, sn, tg, tu, td, tn = call(
        wide(pg), wide(pu), pd[0], pn.reshape(8, 128), mg, mu, md.T, mn.reshape(1, -1), eg, eu, ed.T, en.reshape(1, -1)
    )
    flat = (2 * Z * ROWS, COLS)
    return (cg.reshape(flat), cu.reshape(flat), cd, cn.reshape(-1), sg, su, sd.T, sn[0], tg, tu, td.T, tn[0])


def solution(mesh):
    rows, cols = P(("shift", "replica"), "model"), P(("shift", "model"), "replica")
    vec = P(("shift", "replica"))
    return jax.shard_map(
        on_device,
        mesh=mesh,
        in_specs=(
            P(("shift", "replica"), None, "model"), P(("shift", "replica"), None, "model"), P(("shift", "replica"), "model", None),
            P(("shift", "replica"), None), rows, rows, cols, vec, rows, rows, cols, vec,
        ),
        out_specs=(
            P("shift", "model"), P("shift", "model"), P(("shift", "model"), None), P("shift"),
            rows, rows, cols, vec, rows, rows, cols, vec,
        ),
        check_vma=False,
    )
```

time: 72 us -> 64.7 us (0.90)
  Pallas kernels: 71.2 us -> 64 us
    pallas_call x1, Pallas kernels: 68.5 us -> 61.3 us  [call(): pl.pallas_call(kernel, out_shape=outs, in_specs=[hbm] * len(args), out_sp...]
where the time goes in v3:
time: 64.7 us; the launch traced here: 64.6 us
  Pallas kernels  64 us (99%)
  between operations  0.66 us (1%)
    pallas_call x1, Pallas kernels, call(): pl.pallas_call(kernel, out_shape=outs, in_specs=[hbm] * len(args), out_sp...  61.3 us
    pallas_call x1, Pallas kernels, call(): pl.pallas_call(write, out_shape=outs[:2] + (S((2 * HALF, 128 * Z), BF16),...  2.65 us

profile of v3, /device:TPU:1, one launch (start us, length us, event | category | flops | bytes accessed | tf_op | source)
XLA Modules:
  0.0 64.6 jit_solution(15299456489320571003)
XLA Ops:
  0.6 61.3 %shard_map.211 = (bf16[8,2,64,768]{3,2,1,0:T(8,128)(2,1)S(1)}, bf16[8,2,64,768]{3,2,1,0:T(8,128)(2,1)S(1)}, bf16[8,2,384,128]{3,2,1,0:T(8,128)(2,1)S(1)}, bf16[8...) custom-call(f32[8,2,64,768]{3,2,1,0:T(8,128)} %bitcast.15, ...), custom_call_target="tpu_custom_call" | custom-call | tf_op jit(solution)/shard_map/pallas_call | solution.py:436
  62.0 2.7 %shard_map.212 = (bf16[8,2,64,768]{3,2,1,0:T(8,128)(2,1)}, bf16[8,2,64,768]{3,2,1,0:T(8,128)(2,1)}, bf16[768,1024]{1,0:T(8,128)(2,1)}, bf16[8,128]{1,0:T(8,128)(...) custom-call(bf16[8,2,64,768]{3,2,1,0:T(8,128)(2,1)S(1)} %get-tuple-e, ...), custom_call_target="tpu_custom_call" | custom-call | tf_op jit(solution)/shard_map/pallas_call | solution.py:444
